TPU v7x, 32 devices: a whole 2x2x4 slice. The times are simulated.
32 devices in a mesh: tiles: 8 (over z, core), feat: 4 (over y, x).
Axes of the slice: x: 2, y: 2, z: 4, core: 2. Of those that a mesh axis runs over, the one named last changes fastest.
Arguments:
- feats: bfloat16 [256, 256, 128], P('tiles', 'feat'), may hold values from -6 to 6
- weight: bfloat16 [128, 128], P('feat'), may hold values from -0.5 to 0.5
- bias: float32 [128], replicated, may hold values from -3 to 3
- neighbours: int32 [256, 16], P('tiles'), may hold values from 0 to 255, as said below
- counts: int32 [256], P('tiles'), may hold values from 4 to 16, as said below
- adj_words: int32 [256, 16, 24, 256], P('tiles', 'feat'), may hold values from 0 to 2047, as said below
- tile_row: int32 [256], replicated, may hold values from 0 to 255, as said below
Outputs:
- new_feats: bfloat16 [256, 256, 128], P('tiles', 'feat')
Inputs may be any that keep to these rules, and one draw needn't show every extreme that they name: A permutation of the slide's tiles; slide tile s is stored in the same band as its id, tile_row[s] // 32 == s // 32. Slide ids run row by row over a grid of 8 tile columns. If tile_row[s] == r, every neighbours[r, k] lies within 2 grid rows and 2 grid columns of s (grid row = id // 8, column = id % 8). Slots at or past counts[r] hold valid ids that are not used. `counts`: some tile has all 16 slots live in every draw. `adj_words`: word w holds source cells 11 w to 11 w + 10 in its bits 0 to 10; bits for cells 256 and beyond are zero.
All inputs are finite; a program needn't handle non-finite values.
Results may differ from a plain program's by a relative error of at most 0.0031.
Values may be sent and summed in bfloat16 or wider, within the bound.
No kernel may reach another device: no remote copies, remote signals or barrier semaphores. Data moves between devices by JAX's collectives and lax.ppermute only.
A program may use at most 64 MiB of HBM per device.

v0:
```python
import functools

import jax
import jax.numpy as jnp
import numpy as np
from jax import lax
from jax.experimental import pallas as pl
from jax.experimental.pallas import tpu as pltpu
from jax.sharding import PartitionSpec as P

BITS = 11
LANES = 128
SUB = 8
REACH = 16


HBM = pl.BlockSpec(memory_space=pltpu.HBM)
SMEM = pl.BlockSpec(memory_space=pltpu.SMEM)
VMEM = pl.BlockSpec(memory_space=pltpu.VMEM)


def row_cells(words, cells):
    spare = words * BITS - cells
    assert spare == SUB and words % SUB == 0
    last, tail = BITS - spare, words - SUB
    order = [(b, w) for b in range(BITS) for w in range(tail)]
    order += [(b, w) for b in range(BITS - 1) for w in range(tail, words)]
    out = []
    for b, w in order:
        moved = w == words - 1 and b >= last
        out.append((tail + b - last) * BITS + BITS - 1 if moved else w * BITS + b)
    assert sorted(out) == list(range(cells))
    return np.array(out, dtype=np.int32)


def pack_kernel(group, dst, per_row, last, sizes, counts_ref, words_ref, *out_refs):
    me = lax.axis_index("feat")
    tiles, slots, words, cells = words_ref.shape
    rows = tiles // per_row
    lane = lax.broadcasted_iota(jnp.int32, (words, LANES), 1)
    sub = lax.broadcasted_iota(jnp.int32, (SUB, cells), 0)

    def row_of(rank, at, c, g, carry):
        for k in range(slots):
            packed = []
            for i in range(per_row):
                tile = g * per_row + i
                live = rank * slots + k < counts_ref[pl.program_id(0) * tiles + tile]
                both = jnp.where(live, words_ref[tile, k], 0)
                tail = both[words - SUB :]
                top = ((tail >> (BITS - 1)) & 1) << (sub + last)
                moved = jnp.sum(top, axis=0, keepdims=True)
                kept = tail & ((1 << (BITS - 1)) - 1)
                tail = jnp.where(sub == SUB - 1, kept | moved, kept)
                packed.append(jnp.concatenate([both[: words - SUB], tail], axis=0))
            for m in range(group):
                start = (rank ^ m) * dst
                block, offset = start // LANES, start % LANES
                row = None
                for i in range(per_row):
                    piece = packed[i][:, block * LANES : (block + 1) * LANES]
                    shift = (i * dst + LANES - offset) % LANES
                    if shift:
                        piece = pltpu.roll(piece, shift, 1)
                    row = piece if row is None else jnp.where(lane >= i * dst, piece, row)
                out_refs[c * group + m][at + g, k] = row.astype(jnp.int16)
        return carry

    for rank in range(group):
        at = 0
        for c, size in enumerate(sizes):
            first, step = at // rows, pl.program_id(0)

            @pl.when((me == rank) & (step >= first) & (step < first + size // rows))
            def _(rank=rank, c=c, first=first):
                lax.fori_loop(0, rows, functools.partial(row_of, rank, (step - first) * rows, c), 0, unroll=min(rows, 4))

            at += size


def prepare_kernel(plan, order_ref, perm_ref, *refs):
    pieces, (low_ref, high_ref, held, sem) = refs[: len(plan)], refs[len(plan) :]
    copies = []
    for n, (m, start) in enumerate(plan):
        ref = pieces[n]
        copies.append(pltpu.make_async_copy(ref, held.at[m, pl.ds(start, ref.shape[0])], sem.at[n]))
    for c in copies:
        c.start()
    for c in copies:
        c.wait()
    perm = perm_ref[...]
    half = low_ref.shape[0]

    def put(out_ref, base):
        def step(i, carry):
            tiles = []
            for j in range(2):
                row = order_ref[base + 2 * i + j]
                tiles.append(jnp.concatenate([held[m, row] for m in range(held.shape[0])], axis=0))
            got = jnp.dot(perm, jnp.concatenate(tiles, axis=1), preferred_element_type=jnp.float32)
            for j in range(2):
                out_ref[2 * i + j] = got[:, j * LANES : (j + 1) * LANES].astype(jnp.bfloat16)
            return carry

        lax.fori_loop(0, half // 2, step, 0, unroll=4)

    put(low_ref, 0)
    put(high_ref, half)


def main_kernel(group, dst, per_row, *refs):
    rows = refs[-1].shape[0] - 1
    batch = min(4, rows // 2)
    sets = [[[pltpu.ACC(q)((2 * dst, 2 * LANES), jnp.float32) for _ in range(per_row // 2)] for _ in range(2)] for q in range(2)]
    linear = [pltpu.ACC(q)((batch * LANES, 2 * LANES), jnp.float32) for q in range(2)]
    pl.run_scoped(lambda a, b: main_body(group, dst, per_row, batch, a, b, *refs), sets, linear)


def main_body(group, dst, per_row, batch, accs, products, src_ref, *refs):
    *ins, weight_ref, bias_ref, out_ref, held, words_all, feats_all, sem, sums_ref, degrees_ref = refs
    half = ins[0].shape[0]
    copies = [(ref, held.at[pl.ds(n * half, half)]) for n, ref in enumerate(ins[:4])]
    copies.append((ins[4], feats_all))
    starts = [0] * group
    for n, ref in enumerate(ins[5:]):
        m = n % group
        copies.append((ref, words_all.at[m, pl.ds(starts[m], ref.shape[0])]))
        starts[m] += ref.shape[0]
    copies = [pltpu.make_async_copy(a, b, sem.at[n]) for n, (a, b) in enumerate(copies)]
    for c in copies:
        c.start()
    for a in [a for by_mxu in accs for by_set in by_mxu for a in by_set] + products:
        pltpu.matmul_pop(a)
    for c in copies:
        c.wait()
    me = lax.axis_index("feat")
    rows, slots, words = words_all.shape[1:4]
    all_slots = group * slots
    bias = bias_ref[...]
    features = bias.shape[1]
    pairs = per_row // 2
    one, zero = jnp.bfloat16(1), jnp.bfloat16(0)
    upper = lax.broadcasted_iota(jnp.int32, (2 * SUB, LANES), 0) >= SUB
    bits = [jnp.where(upper, 2 << b, 1 << b).astype(jnp.int16) for b in range(0, BITS - 1, 2)]

    def finished(which):
        got = [pltpu.matmul_pop(accs[0][which][p]) + pltpu.matmul_pop(accs[1][which][p]) for p in range(pairs)]
        return jnp.concatenate(
            [s[j * dst : (j + 1) * dst, j * features : (j + 1) * features] for s in got for j in range(2)], axis=0
        )

    def row_of(row, which):
        tile = row * per_row
        count = jnp.zeros((SUB, LANES), jnp.int32)
        turn = 0
        for m in range(group):
            for k in range(slots):
                slot = (me ^ m) * slots + k
                parts = [words_all[m, row, k, w : w + SUB] for w in range(0, words, SUB)]
                for part in parts:
                    count = count + lax.population_count(part.astype(jnp.int32))
                front = jnp.concatenate(parts[:-1], axis=0)
                back = jnp.concatenate([parts[-1]] * 2, axis=0)
                planes = [jnp.where((front & jnp.int16(1 << b)) != 0, one, zero) for b in range(BITS)]
                planes += [jnp.where((back & bit) != 0, one, zero) for bit in bits]
                mask = jnp.concatenate(planes, axis=0).T
                mxu = turn % 2
                for p in range(pairs):
                    s0 = src_ref[(tile + 2 * p) * all_slots + slot]
                    s1 = src_ref[(tile + 2 * p + 1) * all_slots + slot]
                    register = (turn // 2 * pairs + p) % 2
                    pltpu.matmul_push_rhs(jnp.concatenate([held[s0], held[s1]], axis=1), register, mxu)
                    part = mask[2 * p * dst : 2 * (p + 1) * dst]
                    pltpu.matmul_acc_lhs(accs[mxu][which][p], part, load_staged_rhs=register)
                turn += 1
                if turn == 6:
                    sums_ref[row] = finished(1 - which)
        degrees_ref[row] = jnp.broadcast_to(jnp.sum(count, axis=0, keepdims=True), (SUB, LANES)).astype(jnp.float32)

    def step(n, carry):
        for j in range(2):
            row_of(2 * n + j, j)
        return carry

    lax.fori_loop(0, rows // 2, step, 0)
    sums_ref[rows] = finished(1)

    for q in range(2):
        pltpu.matmul_push_rhs(weight_ref[...], 0, q)
    for n in range(0, rows, batch):
        q = n // batch % 2
        bases, wide = [], []
        for row in range(n, n + batch):
            scale = jnp.sqrt(degrees_ref[row] + 1.0).T[:, :1]
            base = feats_all[row * per_row : (row + 1) * per_row].reshape(LANES, features).astype(jnp.float32)
            normed = ((sums_ref[row + 1] + base) / scale).astype(jnp.bfloat16)
            bases.append(base)
            wide.append(jnp.concatenate([normed, jnp.zeros_like(normed)], axis=1))
        pltpu.matmul_acc_lhs(products[q], jnp.concatenate(wide, axis=0), load_staged_rhs=0 if n // batch < 2 else None)
        linear = pltpu.matmul_pop(products[q])[:, :features] + bias
        result = (jnp.concatenate(bases, axis=0) + jnp.maximum(linear, 0.0)).astype(jnp.bfloat16)
        out_ref[n * per_row : (n + batch) * per_row] = result.reshape(batch * per_row, dst, features)


def swap(x, group, m):
    return lax.ppermute(x, "feat", [(i, i ^ m) for i in range(group)])


def gathered(x, group):
    half = x.shape[0] // 2
    direct = [1 << n for n in range(group.bit_length() - 1)]
    whole = {0: [(0, x)]} | {m: [(0, swap(x, group, m))] for m in direct}
    for m in range(1, group):
        bits = [bit for bit in direct if m & bit]
        if len(bits) > 1:
            whole[m] = [
                (start, swap(part[start : start + half] if part.shape[0] > half else part, group, bit))
                for start, bit in ((0, bits[-1]), (half, bits[0]))
                for at, part in whole[m ^ bit]
                if at <= start < at + part.shape[0]
            ]
    return whole


def per_device(feats, weight, bias, neighbours, counts, adj_words, tile_row):
    group, bands = lax.axis_size("feat"), lax.axis_size("tiles")
    me, rank = lax.axis_index("feat"), lax.axis_index("tiles")
    tiles, dst, features = feats.shape
    _, slots, words, cells = adj_words.shape
    half = tiles // 2
    per_row = LANES // dst
    assert half >= REACH and tiles % per_row == 0 and per_row % 2 == 0 and features == LANES
    rows = tiles // per_row
    sizes = [rows // 4, rows - rows // 4]
    first_tile = rank * tiles

    shapes = [jax.ShapeDtypeStruct((n, slots, words, LANES), jnp.int16) for n in sizes for _ in range(group)]
    block = min(sizes) * per_row
    packed = pl.pallas_call(
        lambda *refs: pack_kernel(group, dst, per_row, BITS - (words * BITS - cells), sizes, *refs),
        out_shape=shapes,
        grid=(tiles // block,),
        in_specs=[SMEM, pl.BlockSpec((block, slots, words, cells), lambda i: (i, 0, 0, 0))],
        out_specs=[pl.BlockSpec(s.shape, lambda i: (0, 0, 0, 0)) for s in shapes],
        cost_estimate=pl.CostEstimate(flops=3 * 10**9, bytes_accessed=5 * 10**6, transcendentals=0),
        name="pack",
    )(counts, adj_words)

    pieces = gathered(feats, group)
    exchanged = []
    for c in range(len(sizes)):
        parts = packed[c * group : (c + 1) * group]
        exchanged += [parts[0]] + [swap(parts[m], group, m) for m in range(1, group)]
    weight_pieces = [weight] + [swap(weight, group, m) for m in range(1, group)]
    weight_full = jnp.stack(weight_pieces)[jnp.arange(group) ^ me].reshape(-1, features)
    weight_wide = jnp.pad(weight_full, ((0, LANES), (0, LANES)))

    order = lax.dynamic_slice_in_dim(tile_row, first_tile, tiles, 0) - first_tile
    cell = row_cells(words, cells)
    column = ((cell // dst) ^ me) * dst + cell % dst
    perm = (column[:, None] == jnp.arange(cells, dtype=jnp.int32)[None, :]).astype(jnp.bfloat16)
    plan = [(m, start) for m in range(group) for start, _ in pieces[m]]
    flat = [part for m in range(group) for _, part in pieces[m]]
    side = jax.ShapeDtypeStruct((half, cells, features), jnp.bfloat16)
    low, high = pl.pallas_call(
        lambda *refs: prepare_kernel(plan, *refs),
        out_shape=[side, side],
        in_specs=[SMEM, VMEM] + [HBM] * len(flat),
        out_specs=[VMEM, VMEM],
        scratch_shapes=[
            pltpu.VMEM((group, tiles, dst, features), jnp.bfloat16),
            pltpu.SemaphoreType.DMA((len(flat),)),
        ],
        cost_estimate=pl.CostEstimate(flops=3 * 10**9, bytes_accessed=4 * 10**6, transcendentals=0),
        name="prepare",
    )(order, perm, *flat)
    up = [(i, i + 1) for i in range(bands - 1)]
    before = lax.ppermute(high, "tiles", up)
    after = lax.ppermute(low, "tiles", [(j, i) for i, j in up])

    source = jnp.clip(neighbours - (first_tile - half), 0, 2 * tiles - 1).reshape(-1)
    return pl.pallas_call(
        lambda *refs: main_kernel(group, dst, per_row, *refs),
        out_shape=jax.ShapeDtypeStruct(feats.shape, feats.dtype),
        in_specs=[SMEM] + [HBM] * (5 + len(exchanged)) + [VMEM] * 2,
        out_specs=VMEM,
        scratch_shapes=[
            pltpu.VMEM((4 * half, cells, features), jnp.bfloat16),
            pltpu.VMEM((group, rows, slots, words, LANES), jnp.int16),
            pltpu.VMEM(feats.shape, jnp.bfloat16),
            pltpu.SemaphoreType.DMA((5 + len(exchanged),)),
            pltpu.VMEM((rows + 1, LANES, features), jnp.float32),
            pltpu.VMEM((rows + 1, SUB, LANES), jnp.float32),
        ],
        cost_estimate=pl.CostEstimate(flops=10**10, bytes_accessed=10**7, transcendentals=0),
        name="main",
    )(source, before, low, high, after, feats, *exchanged, weight_wide, bias[None, :])


def solution(mesh):
    return jax.shard_map(
        per_device,
        mesh=mesh,
        in_specs=(
            P("tiles", "feat", None),
            P("feat", None),
            P(),
            P("tiles", None),
            P("tiles"),
            P("tiles", "feat", None, None),
            P(),
        ),
        out_specs=P("tiles", "feat", None),
        check_vma=False,
    )
```

profile of v0, /device:TPU:0, one launch (start us, length us, event | category | flops | bytes accessed | tf_op | source)
XLA Modules:
  0.0 74.9 jit_solution(8543052920078719073)
XLA Ops:
  0.0 3.0 %collective-permute-start.1 = (bf16[32,64,128]{2,1,0:T(8,128)(2,1)}, bf16[32,64,128]{2,1,0:T(8,128)(2,1)S(1)}, u32[]{:S(2)}, u32[]{:S(2)}) collective-permute-start(bf16[32,64,128]{2,1,0:T(8,128)(2,1)} %refs_5_.1), channel_id=1, source_target_pairs={{0,2},{1,3},{2,0},{3,1},{4,6},{5,7},{6,4},{7,5},{8,10},{9,11},{10,... | collective-permute-start | bytes 1572872 | tf_op jit(solution)/shard_map/ppermute | solution.py:206
  3.0 1.5 %collective-permute-start = (bf16[32,64,128]{2,1,0:T(8,128)(2,1)}, bf16[32,64,128]{2,1,0:T(8,128)(2,1)S(1)}, u32[]{:S(2)}, u32[]{:S(2)}) collective-permute-start(bf16[32,64,128]{2,1,0:T(8,128)(2,1)} %refs_5_.1), channel_id=1, source_target_pairs={{0,1},{1,0},{2,3},{3,2},{4,5},{5,4},{6,7},{7,6},{8,9},{9,8},{10,11... | collective-permute-start | bytes 1572872 | tf_op jit(solution)/shard_map/ppermute | solution.py:206
  4.5 0.7 multiply_add_fusion
  5.2 9.9 %collective-permute-done.1.refs_4_ = bf16[32,64,128]{2,1,0:T(8,128)(2,1)S(1)} collective-permute-done((bf16[32,64,128]{2,1,0:T(8,128)(2,1)}, bf16[32,64,128]{2,1,0:T(8,128)(2,1)S(1)}, u32[]{:S(2)}, u32[]{:S(2)}) %collective-permute-start.1) | collective-permute-done | bytes 524320 | tf_op jit(solution)/shard_map/ppermute | solution.py:206
  15.2 1.8 %collective-permute-start.3 = (bf16[16,64,128]{2,1,0:T(8,128)(2,1)S(1)}, bf16[16,64,128]{2,1,0:T(8,128)(2,1)S(1)}, u32[]{:S(2)}, u32[]{:S(2)}) collective-permute-start(bf16[16,64,128]{2,1,0:T(8,128)(2,1)S(1)} %slice.11), channel_id=1, source_target_pairs={{0,1},{1,0},{2,3},{3,2},{4,5},{5,4},{6,7},{7,6},{8,9},{9,8},{10,11... | collective-permute-start | bytes 786440 | tf_op jit(solution)/shard_map/ppermute | solution.py:206
  17.0 1.6 %collective-permute-start.2 = (bf16[16,64,128]{2,1,0:T(8,128)(2,1)S(1)}, bf16[16,64,128]{2,1,0:T(8,128)(2,1)S(1)}, u32[]{:S(2)}, u32[]{:S(2)}) collective-permute-start(bf16[16,64,128]{2,1,0:T(8,128)(2,1)S(1)} %slice.10), channel_id=1, source_target_pairs={{0,2},{1,3},{2,0},{3,1},{4,6},{5,7},{6,4},{7,5},{8,10},{9,11},{10,... | collective-permute-start | bytes 786440 | tf_op jit(solution)/shard_map/ppermute | solution.py:206
  18.5 1.3 %dynamic-slice_subtract_fusion.refs_0_ = s32[32]{0:T(128)} fusion(s32[256]{0:T(256)} %param.15, s32[]{:T(128)S(6)} %select_n.13, s32[]{:T(128)S(6)} %mul.9), kind=kLoop, calls=%fused_computation.9 | loop fusion | flops 32 | bytes 264 | tf_op jit(solution)/shard_map/sub | solution.py:258
  19.8 0.7 fusion.refs_1_
  20.6 2.1 %collective-permute-done.3.refs_6_ = bf16[16,64,128]{2,1,0:T(8,128)(2,1)S(1)} collective-permute-done((bf16[16,64,128]{2,1,0:T(8,128)(2,1)S(1)}, bf16[16,64,128]{2,1,0:T(8,128)(2,1)S(1)}, u32[]{:S(2)}, u32[]{:S(2)}) %collective-permute-start.3) | collective-permute-done | bytes 262176 | tf_op jit(solution)/shard_map/ppermute | solution.py:206
  22.7 1.2 %collective-permute-done.2.refs_5_ = bf16[16,64,128]{2,1,0:T(8,128)(2,1)S(1)} collective-permute-done((bf16[16,64,128]{2,1,0:T(8,128)(2,1)S(1)}, bf16[16,64,128]{2,1,0:T(8,128)(2,1)S(1)}, u32[]{:S(2)}, u32[]{:S(2)}) %collective-permute-start.2) | collective-permute-done | bytes 262176 | tf_op jit(solution)/shard_map/ppermute | solution.py:206
  24.0 0.7 copy-done.10
  24.7 4.8 %prepare.1 = (bf16[16,256,128]{2,1,0:T(8,128)(2,1)}, bf16[16,256,128]{2,1,0:T(8,128)(2,1)}) custom-call(s32[32]{0:T(128)} %dynamic-slice_subtract_fusion.refs_0_, bf16[256,256]{1,0:T(8,128)(2,1)} %fusion.refs_1_, bf16[32,64,128]{2,1,0:T(8,128)(2,1)} %refs_5_.1, bf16[32,64,128]{2,1,0:T(8,128)(2,1)} %copy-done.1, bf16[32,64,128]{2,1,0:T(8,128)(2,1)} %copy-done, ...), custom_call_target="tpu_custom_call" | custom-call | flops 3000000000 | bytes 4000000 | tf_op jit(solution)/shard_map/prepare/pallas_call | solution.py:265
  29.5 1.4 %collective-permute-start.4 = (bf16[16,256,128]{2,1,0:T(8,128)(2,1)}, bf16[16,256,128]{2,1,0:T(8,128)(2,1)S(1)}, u32[]{:S(2)}, u32[]{:S(2)}) collective-permute-start(bf16[16,256,128]{2,1,0:T(8,128)(2,1)} %get-tuple-element.15.refs_3_), channel_id=1, source_target_pairs={{0,4},{4,8},{8,12},{12,16},{16,20},{20,24},{24,28},{1,5},{5,9},{9,... | collective-permute-start | bytes 3145736 | tf_op jit(solution)/shard_map/ppermute | solution.py:278
  30.9 1.3 %collective-permute-start.5 = (bf16[16,256,128]{2,1,0:T(8,128)(2,1)}, bf16[16,256,128]{2,1,0:T(8,128)(2,1)S(1)}, u32[]{:S(2)}, u32[]{:S(2)}) collective-permute-start(bf16[16,256,128]{2,1,0:T(8,128)(2,1)} %get-tuple-element.16.refs_2_), channel_id=1, source_target_pairs={{4,0},{8,4},{12,8},{16,12},{20,16},{24,20},{28,24},{5,1},{9,5},{13... | collective-permute-start | bytes 3145736 | tf_op jit(solution)/shard_map/ppermute | solution.py:279
  32.2 1.2 %collective-permute-start.12 = (bf16[32,128]{1,0:T(8,128)(2,1)S(1)}, bf16[32,128]{1,0:T(8,128)(2,1)S(1)}, u32[]{:S(2)}, u32[]{:S(2)}) collective-permute-start(bf16[32,128]{1,0:T(8,128)(2,1)S(1)} %copy-done.3), channel_id=1, source_target_pairs={{0,1},{1,0},{2,3},{3,2},{4,5},{5,4},{6,7},{7,6},{8,9},{9,8},{10,11... | collective-permute-start | bytes 24584 | tf_op jit(solution)/shard_map/ppermute | solution.py:206
  33.4 1.8 %collective-permute-start.14 = (bf16[32,128]{1,0:T(8,128)(2,1)S(1)}, bf16[32,128]{1,0:T(8,128)(2,1)S(1)}, u32[]{:S(2)}, u32[]{:S(2)}) collective-permute-start(bf16[32,128]{1,0:T(8,128)(2,1)S(1)} %copy-done.3), channel_id=1, source_target_pairs={{0,3},{1,2},{2,1},{3,0},{4,7},{5,6},{6,5},{7,4},{8,11},{9,10},{10,... | collective-permute-start | bytes 24584 | tf_op jit(solution)/shard_map/ppermute | solution.py:206
  35.7 4.6 %pack.1 = (s16[4,4,24,128]{3,2,1,0:T(8,128)(2,1)}, s16[4,4,24,128]{3,2,1,0:T(8,128)(2,1)}, s16[4,4,24,128]{3,2,1,0:T(8,128)(2,1)}, s16[4,4,24,128]{3,2,1,0:T(8,1...) custom-call(s32[32]{0:T(128)} %refs_0_.1, ...), custom_call_target="tpu_custom_call" | custom-call | flops 3000000000 | bytes 5000000 | tf_op jit(solution)/shard_map/pack/pallas_call | solution.py:239
  40.3 1.2 %collective-permute-start.6 = (s16[4,4,24,128]{3,2,1,0:T(8,128)(2,1)}, s16[4,4,24,128]{3,2,1,0:T(8,128)(2,1)S(1)}, u32[]{:S(2)}, u32[]{:S(2)}) collective-permute-start(s16[4,4,24,128]{3,2,1,0:T(8,128)(2,1)} %get-tuple-element.18), channel_id=1, source_target_pairs={{0,1},{1,0},{2,3},{3,2},{4,5},{5,4},{6,7},{7,6},{8,9},{9,8},{10,11... | collective-permute-start | bytes 294920 | tf_op jit(solution)/shard_map/ppermute | solution.py:206
  41.5 1.3 %collective-permute-start.7 = (s16[4,4,24,128]{3,2,1,0:T(8,128)(2,1)}, s16[4,4,24,128]{3,2,1,0:T(8,128)(2,1)S(1)}, u32[]{:S(2)}, u32[]{:S(2)}) collective-permute-start(s16[4,4,24,128]{3,2,1,0:T(8,128)(2,1)} %get-tuple-element.19), channel_id=1, source_target_pairs={{0,2},{1,3},{2,0},{3,1},{4,6},{5,7},{6,4},{7,5},{8,10},{9,11},{10,... | collective-permute-start | bytes 294920 | tf_op jit(solution)/shard_map/ppermute | solution.py:206
  42.7 1.1 %collective-permute-start.8 = (s16[4,4,24,128]{3,2,1,0:T(8,128)(2,1)}, s16[4,4,24,128]{3,2,1,0:T(8,128)(2,1)S(1)}, u32[]{:S(2)}, u32[]{:S(2)}) collective-permute-start(s16[4,4,24,128]{3,2,1,0:T(8,128)(2,1)} %get-tuple-element.20), channel_id=1, source_target_pairs={{0,3},{1,2},{2,1},{3,0},{4,7},{5,6},{6,5},{7,4},{8,11},{9,10},{10,... | collective-permute-start | bytes 294920 | tf_op jit(solution)/shard_map/ppermute | solution.py:206
  43.9 0.6 reshape.23.refs_0_
  44.5 0.6 collective-permute-done.6.refs_7_
  45.1 1.1 %collective-permute-start.9 = (s16[12,4,24,128]{3,2,1,0:T(8,128)(2,1)}, s16[12,4,24,128]{3,2,1,0:T(8,128)(2,1)S(1)}, u32[]{:S(2)}, u32[]{:S(2)}) collective-permute-start(s16[12,4,24,128]{3,2,1,0:T(8,128)(2,1)} %get-tuple-element.22), channel_id=1, source_target_pairs={{0,1},{1,0},{2,3},{3,2},{4,5},{5,4},{6,7},{7,6},{8,9},{9,8},{10,11... | collective-permute-start | bytes 884744 | tf_op jit(solution)/shard_map/ppermute | solution.py:206
  46.6 1.3 %collective-permute-start.10 = (s16[12,4,24,128]{3,2,1,0:T(8,128)(2,1)}, s16[12,4,24,128]{3,2,1,0:T(8,128)(2,1)S(1)}, u32[]{:S(2)}, u32[]{:S(2)}) collective-permute-start(s16[12,4,24,128]{3,2,1,0:T(8,128)(2,1)} %get-tuple-element.23), channel_id=1, source_target_pairs={{0,2},{1,3},{2,0},{3,1},{4,6},{5,7},{6,4},{7,5},{8,10},{9,11},{10,... | collective-permute-start | bytes 884744 | tf_op jit(solution)/shard_map/ppermute | solution.py:206
  47.8 1.2 %collective-permute-done.8.refs_9_ = s16[4,4,24,128]{3,2,1,0:T(8,128)(2,1)S(1)} collective-permute-done((s16[4,4,24,128]{3,2,1,0:T(8,128)(2,1)}, s16[4,4,24,128]{3,2,1,0:T(8,128)(2,1)S(1)}, u32[]{:S(2)}, u32[]{:S(2)}) %collective-permute-start.8) | collective-permute-done | bytes 98336 | tf_op jit(solution)/shard_map/ppermute | solution.py:206
  49.0 1.2 %collective-permute-start.11 = (s16[12,4,24,128]{3,2,1,0:T(8,128)(2,1)}, s16[12,4,24,128]{3,2,1,0:T(8,128)(2,1)S(1)}, u32[]{:S(2)}, u32[]{:S(2)}) collective-permute-start(s16[12,4,24,128]{3,2,1,0:T(8,128)(2,1)} %get-tuple-element.24), channel_id=1, source_target_pairs={{0,3},{1,2},{2,1},{3,0},{4,7},{5,6},{6,5},{7,4},{8,11},{9,10},{10,... | collective-permute-start | bytes 884744 | tf_op jit(solution)/shard_map/ppermute | solution.py:206
  50.2 0.6 gather_fusion
  50.8 0.7 pad.4.refs_14_
  51.5 3.6 %collective-permute-done.9.refs_11_ = s16[12,4,24,128]{3,2,1,0:T(8,128)(2,1)S(1)} collective-permute-done((s16[12,4,24,128]{3,2,1,0:T(8,128)(2,1)}, s16[12,4,24,128]{3,2,1,0:T(8,128)(2,1)S(1)}, u32[]{:S(2)}, u32[]{:S(2)}) %collective-permute-start.9) | collective-permute-done | bytes 294944 | tf_op jit(solution)/shard_map/ppermute | solution.py:206
  55.1 7.3 %collective-permute-done.11.refs_13_ = s16[12,4,24,128]{3,2,1,0:T(8,128)(2,1)S(1)} collective-permute-done((s16[12,4,24,128]{3,2,1,0:T(8,128)(2,1)}, s16[12,4,24,128]{3,2,1,0:T(8,128)(2,1)S(1)}, u32[]{:S(2)}, u32[]{:S(2)}) %collective-permute-start.11) | collective-permute-done | bytes 294944 | tf_op jit(solution)/shard_map/ppermute | solution.py:206
  62.5 0.6 copy-done.8
  63.8 11.1 %main.1 = bf16[32,64,128]{2,1,0:T(8,128)(2,1)} custom-call(s32[512]{0:T(512)} %reshape.23.refs_0_, bf16[16,256,128]{2,1,0:T(8,128)(2,1)} %copy-done.4, bf16[16,256,128]{2,1,0:T(8,128)(2,1)} %get-tuple-element.16.refs_2_, bf16[16,256,128]{2,1,0:T(8,128)(2,1)} %get-tuple-element.15.refs_3_, bf16[16,256,128]{2,1,0:T(8,128)(2,1)} %copy-done.5, ...), custom_call_target="tpu_custom_call" | custom-call | flops 10000000000 | bytes 10000000 | tf_op jit(solution)/shard_map/main/pallas_call | solution.py:282
  (42 shorter events, 1.7 us)
Async XLA Ops:
  0.0 15.1 %collective-permute-start.1 = (bf16[32,64,128]{2,1,0:T(8,128)(2,1)}, bf16[32,64,128]{2,1,0:T(8,128)(2,1)S(1)}, u32[]{:S(2)}, u32[]{:S(2)}) collective-permute-start(bf16[32,64,128]{2,1,0:T(8,128)(2,1)} %refs_5_.1), channel_id=1, source_target_pairs={{0,2},{1,3},{2,0},{3,1},{4,6},{5,7},{6,4},{7,5},{8,10},{9,11},{10,... | collective-permute-start | bytes 1572872 | tf_op jit(solution)/shard_map/ppermute | solution.py:206
  3.0 13.9 %collective-permute-start = (bf16[32,64,128]{2,1,0:T(8,128)(2,1)}, bf16[32,64,128]{2,1,0:T(8,128)(2,1)S(1)}, u32[]{:S(2)}, u32[]{:S(2)}) collective-permute-start(bf16[32,64,128]{2,1,0:T(8,128)(2,1)} %refs_5_.1), channel_id=1, source_target_pairs={{0,1},{1,0},{2,3},{3,2},{4,5},{5,4},{6,7},{7,6},{8,9},{9,8},{10,11... | collective-permute-start | bytes 1572872 | tf_op jit(solution)/shard_map/ppermute | solution.py:206
  15.1 8.8 %copy-start = (bf16[32,64,128]{2,1,0:T(8,128)(2,1)}, bf16[32,64,128]{2,1,0:T(8,128)(2,1)S(1)}, u32[]{:S(2)}) copy-start(bf16[32,64,128]{2,1,0:T(8,128)(2,1)S(1)} %collective-permute-done.1.refs_4_) | copy-start | bytes 1572868
  15.2 7.5 %collective-permute-start.3 = (bf16[16,64,128]{2,1,0:T(8,128)(2,1)S(1)}, bf16[16,64,128]{2,1,0:T(8,128)(2,1)S(1)}, u32[]{:S(2)}, u32[]{:S(2)}) collective-permute-start(bf16[16,64,128]{2,1,0:T(8,128)(2,1)S(1)} %slice.11), channel_id=1, source_target_pairs={{0,1},{1,0},{2,3},{3,2},{4,5},{5,4},{6,7},{7,6},{8,9},{9,8},{10,11... | collective-permute-start | bytes 786440 | tf_op jit(solution)/shard_map/ppermute | solution.py:206
  16.9 7.0 %copy-start.1 = (bf16[32,64,128]{2,1,0:T(8,128)(2,1)}, bf16[32,64,128]{2,1,0:T(8,128)(2,1)S(1)}, u32[]{:S(2)}) copy-start(bf16[32,64,128]{2,1,0:T(8,128)(2,1)S(1)} %collective-permute-done.refs_3_) | copy-start | bytes 1572868
  17.0 7.0 %collective-permute-start.2 = (bf16[16,64,128]{2,1,0:T(8,128)(2,1)S(1)}, bf16[16,64,128]{2,1,0:T(8,128)(2,1)S(1)}, u32[]{:S(2)}, u32[]{:S(2)}) collective-permute-start(bf16[16,64,128]{2,1,0:T(8,128)(2,1)S(1)} %slice.10), channel_id=1, source_target_pairs={{0,2},{1,3},{2,0},{3,1},{4,6},{5,7},{6,4},{7,5},{8,10},{9,11},{10,... | collective-permute-start | bytes 786440 | tf_op jit(solution)/shard_map/ppermute | solution.py:206
  20.6 11.6 %copy-start.3 = (bf16[32,128]{1,0:T(8,128)(2,1)S(1)}, bf16[32,128]{1,0:T(8,128)(2,1)}, u32[]{:S(2)}) copy-start(bf16[32,128]{1,0:T(8,128)(2,1)} %param.10) | copy-start | bytes 24580
  22.7 1.3 %copy-start.9 = (bf16[16,64,128]{2,1,0:T(8,128)(2,1)}, bf16[16,64,128]{2,1,0:T(8,128)(2,1)S(1)}, u32[]{:S(2)}) copy-start(bf16[16,64,128]{2,1,0:T(8,128)(2,1)S(1)} %collective-permute-done.3.refs_6_) | copy-start | bytes 786436
  23.9 0.7 copy-start.10
  29.5 32.9 %collective-permute-start.4 = (bf16[16,256,128]{2,1,0:T(8,128)(2,1)}, bf16[16,256,128]{2,1,0:T(8,128)(2,1)S(1)}, u32[]{:S(2)}, u32[]{:S(2)}) collective-permute-start(bf16[16,256,128]{2,1,0:T(8,128)(2,1)} %get-tuple-element.15.refs_3_), channel_id=1, source_target_pairs={{0,4},{4,8},{8,12},{12,16},{16,20},{20,24},{24,28},{1,5},{5,9},{9,... | collective-permute-start | bytes 3145736 | tf_op jit(solution)/shard_map/ppermute | solution.py:278
  30.9 13.0 %copy-start.2 = (s32[32,16]{0,1:T(8,128)S(1)}, s32[32,16]{0,1:T(8,128)}, u32[]{:S(2)}) copy-start(s32[32,16]{0,1:T(8,128)} %param.12) | copy-start | bytes 6148
  30.9 31.5 %collective-permute-start.5 = (bf16[16,256,128]{2,1,0:T(8,128)(2,1)}, bf16[16,256,128]{2,1,0:T(8,128)(2,1)S(1)}, u32[]{:S(2)}, u32[]{:S(2)}) collective-permute-start(bf16[16,256,128]{2,1,0:T(8,128)(2,1)} %get-tuple-element.16.refs_2_), channel_id=1, source_target_pairs={{4,0},{8,4},{12,8},{16,12},{20,16},{24,20},{28,24},{5,1},{9,5},{13... | collective-permute-start | bytes 3145736 | tf_op jit(solution)/shard_map/ppermute | solution.py:279
  32.2 8.1 %collective-permute-start.12 = (bf16[32,128]{1,0:T(8,128)(2,1)S(1)}, bf16[32,128]{1,0:T(8,128)(2,1)S(1)}, u32[]{:S(2)}, u32[]{:S(2)}) collective-permute-start(bf16[32,128]{1,0:T(8,128)(2,1)S(1)} %copy-done.3), channel_id=1, source_target_pairs={{0,1},{1,0},{2,3},{3,2},{4,5},{5,4},{6,7},{7,6},{8,9},{9,8},{10,11... | collective-permute-start | bytes 24584 | tf_op jit(solution)/shard_map/ppermute | solution.py:206
  33.4 8.1 %collective-permute-start.14 = (bf16[32,128]{1,0:T(8,128)(2,1)S(1)}, bf16[32,128]{1,0:T(8,128)(2,1)S(1)}, u32[]{:S(2)}, u32[]{:S(2)}) collective-permute-start(bf16[32,128]{1,0:T(8,128)(2,1)S(1)} %copy-done.3), channel_id=1, source_target_pairs={{0,3},{1,2},{2,1},{3,0},{4,7},{5,6},{6,5},{7,4},{8,11},{9,10},{10,... | collective-permute-start | bytes 24584 | tf_op jit(solution)/shard_map/ppermute | solution.py:206
  35.2 7.5 %collective-permute-start.13 = (bf16[32,128]{1,0:T(8,128)(2,1)S(1)}, bf16[32,128]{1,0:T(8,128)(2,1)S(1)}, u32[]{:S(2)}, u32[]{:S(2)}) collective-permute-start(bf16[32,128]{1,0:T(8,128)(2,1)S(1)} %copy-done.3), channel_id=1, source_target_pairs={{0,2},{1,3},{2,0},{3,1},{4,6},{5,7},{6,4},{7,5},{8,10},{9,11},{10,... | collective-permute-start | bytes 24584 | tf_op jit(solution)/shard_map/ppermute | solution.py:206
  40.3 4.8 %collective-permute-start.6 = (s16[4,4,24,128]{3,2,1,0:T(8,128)(2,1)}, s16[4,4,24,128]{3,2,1,0:T(8,128)(2,1)S(1)}, u32[]{:S(2)}, u32[]{:S(2)}) collective-permute-start(s16[4,4,24,128]{3,2,1,0:T(8,128)(2,1)} %get-tuple-element.18), channel_id=1, source_target_pairs={{0,1},{1,0},{2,3},{3,2},{4,5},{5,4},{6,7},{7,6},{8,9},{9,8},{10,11... | collective-permute-start | bytes 294920 | tf_op jit(solution)/shard_map/ppermute | solution.py:206
  41.5 5.1 %collective-permute-start.7 = (s16[4,4,24,128]{3,2,1,0:T(8,128)(2,1)}, s16[4,4,24,128]{3,2,1,0:T(8,128)(2,1)S(1)}, u32[]{:S(2)}, u32[]{:S(2)}) collective-permute-start(s16[4,4,24,128]{3,2,1,0:T(8,128)(2,1)} %get-tuple-element.19), channel_id=1, source_target_pairs={{0,2},{1,3},{2,0},{3,1},{4,6},{5,7},{6,4},{7,5},{8,10},{9,11},{10,... | collective-permute-start | bytes 294920 | tf_op jit(solution)/shard_map/ppermute | solution.py:206
  42.7 6.3 %collective-permute-start.8 = (s16[4,4,24,128]{3,2,1,0:T(8,128)(2,1)}, s16[4,4,24,128]{3,2,1,0:T(8,128)(2,1)S(1)}, u32[]{:S(2)}, u32[]{:S(2)}) collective-permute-start(s16[4,4,24,128]{3,2,1,0:T(8,128)(2,1)} %get-tuple-element.20), channel_id=1, source_target_pairs={{0,3},{1,2},{2,1},{3,0},{4,7},{5,6},{6,5},{7,4},{8,11},{9,10},{10,... | collective-permute-start | bytes 294920 | tf_op jit(solution)/shard_map/ppermute | solution.py:206
  45.1 17.3 %copy-start.11 = (s16[4,4,24,128]{3,2,1,0:T(8,128)(2,1)}, s16[4,4,24,128]{3,2,1,0:T(8,128)(2,1)S(1)}, u32[]{:S(2)}) copy-start(s16[4,4,24,128]{3,2,1,0:T(8,128)(2,1)S(1)} %collective-permute-done.6.refs_7_) | copy-start | bytes 294916
  45.1 9.9 %collective-permute-start.9 = (s16[12,4,24,128]{3,2,1,0:T(8,128)(2,1)}, s16[12,4,24,128]{3,2,1,0:T(8,128)(2,1)S(1)}, u32[]{:S(2)}, u32[]{:S(2)}) collective-permute-start(s16[12,4,24,128]{3,2,1,0:T(8,128)(2,1)} %get-tuple-element.22), channel_id=1, source_target_pairs={{0,1},{1,0},{2,3},{3,2},{4,5},{5,4},{6,7},{7,6},{8,9},{9,8},{10,11... | collective-permute-start | bytes 884744 | tf_op jit(solution)/shard_map/ppermute | solution.py:206
  46.6 15.9 %copy-start.12 = (s16[4,4,24,128]{3,2,1,0:T(8,128)(2,1)}, s16[4,4,24,128]{3,2,1,0:T(8,128)(2,1)S(1)}, u32[]{:S(2)}) copy-start(s16[4,4,24,128]{3,2,1,0:T(8,128)(2,1)S(1)} %collective-permute-done.7.refs_8_) | copy-start | bytes 294916
  46.6 8.5 %collective-permute-start.10 = (s16[12,4,24,128]{3,2,1,0:T(8,128)(2,1)}, s16[12,4,24,128]{3,2,1,0:T(8,128)(2,1)S(1)}, u32[]{:S(2)}, u32[]{:S(2)}) collective-permute-start(s16[12,4,24,128]{3,2,1,0:T(8,128)(2,1)} %get-tuple-element.23), channel_id=1, source_target_pairs={{0,2},{1,3},{2,0},{3,1},{4,6},{5,7},{6,4},{7,5},{8,10},{9,11},{10,... | collective-permute-start | bytes 884744 | tf_op jit(solution)/shard_map/ppermute | solution.py:206
  49.0 13.4 %copy-start.13 = (s16[4,4,24,128]{3,2,1,0:T(8,128)(2,1)}, s16[4,4,24,128]{3,2,1,0:T(8,128)(2,1)S(1)}, u32[]{:S(2)}) copy-start(s16[4,4,24,128]{3,2,1,0:T(8,128)(2,1)S(1)} %collective-permute-done.8.refs_9_) | copy-start | bytes 294916
  49.0 13.4 %collective-permute-start.11 = (s16[12,4,24,128]{3,2,1,0:T(8,128)(2,1)}, s16[12,4,24,128]{3,2,1,0:T(8,128)(2,1)S(1)}, u32[]{:S(2)}, u32[]{:S(2)}) collective-permute-start(s16[12,4,24,128]{3,2,1,0:T(8,128)(2,1)} %get-tuple-element.24), channel_id=1, source_target_pairs={{0,3},{1,2},{2,1},{3,0},{4,7},{5,6},{6,5},{7,4},{8,11},{9,10},{10,... | collective-permute-start | bytes 884744 | tf_op jit(solution)/shard_map/ppermute | solution.py:206
  55.0 7.4 %copy-start.6 = (s16[12,4,24,128]{3,2,1,0:T(8,128)(2,1)}, s16[12,4,24,128]{3,2,1,0:T(8,128)(2,1)S(1)}, u32[]{:S(2)}) copy-start(s16[12,4,24,128]{3,2,1,0:T(8,128)(2,1)S(1)} %collective-permute-done.9.refs_11_) | copy-start | bytes 884740
  55.1 7.4 %copy-start.7 = (s16[12,4,24,128]{3,2,1,0:T(8,128)(2,1)}, s16[12,4,24,128]{3,2,1,0:T(8,128)(2,1)S(1)}, u32[]{:S(2)}) copy-start(s16[12,4,24,128]{3,2,1,0:T(8,128)(2,1)S(1)} %collective-permute-done.10.refs_12_) | copy-start | bytes 884740
  62.4 0.7 copy-start.8
  62.4 1.1 %copy-start.4 = (bf16[16,256,128]{2,1,0:T(8,128)(2,1)}, bf16[16,256,128]{2,1,0:T(8,128)(2,1)S(1)}, u32[]{:S(2)}) copy-start(bf16[16,256,128]{2,1,0:T(8,128)(2,1)S(1)} %collective-permute-done.4.refs_1_) | copy-start | bytes 3145732
  62.4 1.4 %copy-start.5 = (bf16[16,256,128]{2,1,0:T(8,128)(2,1)}, bf16[16,256,128]{2,1,0:T(8,128)(2,1)S(1)}, u32[]{:S(2)}) copy-start(bf16[16,256,128]{2,1,0:T(8,128)(2,1)S(1)} %collective-permute-done.5.refs_4_) | copy-start | bytes 3145732
where the time goes:
time: 75.2 us; the launch traced here: 74.9 us
  waiting for transfers between devices  26.3 us (35%)
  starting transfers between devices  21.1 us (28%)
  Pallas kernels  20.5 us (27%)
  local copies, waits for them, and re-layouts  4.04 us (5%)
  other arithmetic  2.74 us (4%)
    ppermute x13, waiting for transfers between devices, swap(): return lax.ppermute(x, 'feat', [(i, i ^ m) for i in range(group)])  26.3 us
    ppermute x13, starting transfers between devices, swap(): return lax.ppermute(x, 'feat', [(i, i ^ m) for i in range(group)])  18.5 us
    pallas_call x1, Pallas kernels, per_device(): pl.pallas_call(lambda *refs: main_kernel(group, dst, per_row, *refs), out...  11.1 us
    pallas_call x1, Pallas kernels, per_device(): pl.pallas_call(lambda *refs: prepare_kernel(plan, *refs), out_shape=[side...  4.81 us
    pallas_call x1, Pallas kernels, per_device(): pl.pallas_call(lambda *refs: pack_kernel(group, dst, per_row, BITS - (wor...  4.57 us
    unnamed x28, local copies, waits for them, and re-layouts  2.07 us
  transfers between devices with their start and end apart: 15, of which 9 were waited for; matrix products, arithmetic and copies ran while one was open for 6% of the time, Pallas kernels for 6%

commit v1 on v0

v1 whole, which is shorter than its diff:
```python
import functools

import jax
import jax.numpy as jnp
import numpy as np
from jax import lax
from jax.experimental import pallas as pl
from jax.experimental.pallas import tpu as pltpu
from jax.sharding import PartitionSpec as P

BITS = 11
LANES = 128
SUB = 8
REACH = 16


HBM = pl.BlockSpec(memory_space=pltpu.HBM)
SMEM = pl.BlockSpec(memory_space=pltpu.SMEM)
VMEM = pl.BlockSpec(memory_space=pltpu.VMEM)


def row_cells(words, cells):
    spare = words * BITS - cells
    assert spare == SUB and words % SUB == 0
    last, tail = BITS - spare, words - SUB
    order = [(b, w) for b in range(BITS) for w in range(tail)]
    order += [(b, w) for b in range(BITS - 1) for w in range(tail, words)]
    out = []
    for b, w in order:
        moved = w == words - 1 and b >= last
        out.append((tail + b - last) * BITS + BITS - 1 if moved else w * BITS + b)
    assert sorted(out) == list(range(cells))
    return np.array(out, dtype=np.int32)


def pack_kernel(group, dst, per_row, last, sizes, counts_ref, words_ref, *out_refs):
    me = lax.axis_index("feat")
    tiles, slots, words, cells = words_ref.shape
    rows = tiles // per_row
    lane = lax.broadcasted_iota(jnp.int32, (words, LANES), 1)
    sub = lax.broadcasted_iota(jnp.int32, (SUB, cells), 0)

    def row_of(rank, at, c, g, carry):
        for k in range(slots):
            packed = []
            for i in range(per_row):
                tile = g * per_row + i
                live = rank * slots + k < counts_ref[pl.program_id(0) * tiles + tile]
                both = jnp.where(live, words_ref[tile, k], 0)
                tail = both[words - SUB :]
                top = ((tail >> (BITS - 1)) & 1) << (sub + last)
                moved = jnp.sum(top, axis=0, keepdims=True)
                kept = tail & ((1 << (BITS - 1)) - 1)
                tail = jnp.where(sub == SUB - 1, kept | moved, kept)
                packed.append(jnp.concatenate([both[: words - SUB], tail], axis=0))
            for m in range(group):
                start = (rank ^ m) * dst
                block, offset = start // LANES, start % LANES
                row = None
                for i in range(per_row):
                    piece = packed[i][:, block * LANES : (block + 1) * LANES]
                    shift = (i * dst + LANES - offset) % LANES
                    if shift:
                        piece = pltpu.roll(piece, shift, 1)
                    row = piece if row is None else jnp.where(lane >= i * dst, piece, row)
                out_refs[c * group + m][at + g, k] = row.astype(jnp.int16)
        return carry

    for rank in range(group):
        at = 0
        for c, size in enumerate(sizes):
            first, step = at // rows, pl.program_id(0)

            @pl.when((me == rank) & (step >= first) & (step < first + size // rows))
            def _(rank=rank, c=c, first=first):
                lax.fori_loop(0, rows, functools.partial(row_of, rank, (step - first) * rows, c), 0, unroll=max(1, min(rows, 16 // group)))

            at += size


def arrange_kernel(near, inner_bits, outer_bits, tiles_ref, *refs):
    pieces, outs = refs[:near], list(refs[near:])
    tiles = pieces[0].shape[0]
    half = tiles // 2
    first = lax.axis_index("tiles") * tiles
    odd = lax.axis_index("tiles") % 2
    for side, bits in ((1 - odd, inner_bits), (odd, outer_bits)):
        together = outs.pop(0)
        alone = {n: outs.pop(0) for n in bits}
        for i in range(half):
            row = tiles_ref[first + side * half + i] - first
            for n in range(near):
                tile = pieces[n][row]
                together[n, i] = tile
                if n in alone:
                    alone[n][i] = tile


def assemble_kernel(group, places, perm_ref, *refs):
    perm = perm_ref[...]
    odd = lax.axis_index("tiles") % 2
    near = [0] + [1 << n for n in range(group.bit_length() - 1)]
    far = [m for m in range(group) if m not in near]
    per_side = 1 + len(far)
    tiles_ref = refs[2 * per_side + group] if len(refs) > 2 * per_side + group else refs[-1]

    def step(base, side, i, carry):
        pair = []
        for j in range(2):
            tile = 2 * i + j
            cut = {m: side[0][n, tile] for n, m in enumerate(near)} | {m: side[1 + n][tile] for n, m in enumerate(far)}
            pair.append(jnp.concatenate([cut[m] for m in range(group)], axis=0))
        got = jnp.dot(perm, jnp.concatenate(pair, axis=1), preferred_element_type=jnp.float32)
        for j in range(2):
            tiles_ref[base + 2 * i + j] = got[:, j * LANES : (j + 1) * LANES].astype(jnp.bfloat16)
        return carry

    for n, (even_place, odd_place) in enumerate(places):
        side = refs[n * per_side : (n + 1) * per_side]
        half = side[0].shape[1]
        base = jnp.where(odd == 1, odd_place * half, even_place * half)
        lax.fori_loop(0, half // 2, functools.partial(step, base, side), 0, unroll=4)
    if tiles_ref is not refs[-1]:
        weights, weight_ref = refs[2 * per_side : 2 * per_side + group], refs[-1]
        me = lax.axis_index("feat")
        _, features = weights[0].shape
        rows = []
        for rank in range(group):
            row = weights[0][...].astype(jnp.float32)
            for m in range(1, group):
                row = jnp.where(me ^ m == rank, weights[m][...].astype(jnp.float32), row)
            rows.append(row)
        weight_ref[...] = jnp.zeros_like(weight_ref)
        weight_ref[:features, :features] = jnp.concatenate(rows, axis=0).astype(jnp.bfloat16)


def main_kernel(group, dst, per_row, *refs):
    rows = refs[-1].shape[0] - 1
    batch = min(4, rows // 2)
    sets = [[[pltpu.ACC(q)((2 * dst, 2 * LANES), jnp.float32) for _ in range(per_row // 2)] for _ in range(2)] for q in range(2)]
    linear = [pltpu.ACC(q)((batch * LANES, 2 * LANES), jnp.float32) for q in range(2)]
    pl.run_scoped(lambda a, b: main_body(group, dst, per_row, batch, a, b, *refs), sets, linear)


def main_body(group, dst, per_row, batch, accs, products, neighbours_ref, *refs):
    held, weight_ref, bias_ref, feats_ref, *ins, out_ref, sums_ref, degrees_ref = refs
    chunk_refs = [ins[n : n + group] for n in range(0, len(ins), group)]
    for a in [a for by_mxu in accs for by_set in by_mxu for a in by_set] + products:
        pltpu.matmul_pop(a)
    me = lax.axis_index("feat")
    rows = sums_ref.shape[0] - 1
    slots, words = ins[0].shape[1:3]
    tiles, half = neighbours_ref.shape[1], held.shape[0] // 4
    origin = lax.axis_index("tiles") * tiles - half
    bias = bias_ref[...]
    features = bias.shape[1]
    pairs = per_row // 2
    one, zero = jnp.bfloat16(1), jnp.bfloat16(0)
    upper = lax.broadcasted_iota(jnp.int32, (2 * SUB, LANES), 0) >= SUB
    bits = [jnp.where(upper, 2 << b, 1 << b).astype(jnp.int16) for b in range(0, BITS - 1, 2)]

    def source(slot, tile):
        return jnp.clip(neighbours_ref[slot, tile] - origin, 0, 4 * half - 1)

    def finished(which):
        got = [pltpu.matmul_pop(accs[0][which][p]) + pltpu.matmul_pop(accs[1][which][p]) for p in range(pairs)]
        return jnp.concatenate(
            [s[j * dst : (j + 1) * dst, j * features : (j + 1) * features] for s in got for j in range(2)], axis=0
        )

    def row_of(words_refs, first, row, which):
        tile = row * per_row
        count = jnp.zeros((SUB, LANES), jnp.int32)
        turn = 0
        for m in range(group):
            for k in range(slots):
                slot = (me ^ m) * slots + k
                parts = [words_refs[m][row - first, k, w : w + SUB] for w in range(0, words, SUB)]
                for part in parts:
                    count = count + lax.population_count(part.astype(jnp.int32))
                front = jnp.concatenate(parts[:-1], axis=0)
                back = jnp.concatenate([parts[-1]] * 2, axis=0)
                planes = [jnp.where((front & jnp.int16(1 << b)) != 0, one, zero) for b in range(BITS)]
                planes += [jnp.where((back & bit) != 0, one, zero) for bit in bits]
                mask = jnp.concatenate(planes, axis=0).T
                mxu = turn % 2
                for p in range(pairs):
                    s0, s1 = (source(slot, tile + 2 * p + j) for j in range(2))
                    register = (turn // 2 * pairs + p) % 2
                    pltpu.matmul_push_rhs(jnp.concatenate([held[s0], held[s1]], axis=1), register, mxu)
                    part = mask[2 * p * dst : 2 * (p + 1) * dst]
                    pltpu.matmul_acc_lhs(accs[mxu][which][p], part, load_staged_rhs=register)
                turn += 1
                if turn == 6:
                    sums_ref[row] = finished(1 - which)
        degrees_ref[row] = jnp.broadcast_to(jnp.sum(count, axis=0, keepdims=True), (SUB, LANES)).astype(jnp.float32)

    first = 0
    for words_refs in chunk_refs:
        size = words_refs[0].shape[0]

        def step(n, carry, words_refs=words_refs, first=first):
            for j in range(2):
                row_of(words_refs, first, first + 2 * n + j, j)
            return carry

        lax.fori_loop(0, size // 2, step, 0)
        first += size
    sums_ref[rows] = finished(1)

    for q in range(2):
        pltpu.matmul_push_rhs(weight_ref[...], 0, q)
    for n in range(0, rows, batch):
        q = n // batch % 2
        bases, wide = [], []
        for row in range(n, n + batch):
            scale = jnp.sqrt(degrees_ref[row] + 1.0).T[:, :1]
            base = feats_ref[row * per_row : (row + 1) * per_row].reshape(LANES, features).astype(jnp.float32)
            normed = ((sums_ref[row + 1] + base) / scale).astype(jnp.bfloat16)
            bases.append(base)
            wide.append(jnp.concatenate([normed, jnp.zeros_like(normed)], axis=1))
        pltpu.matmul_acc_lhs(products[q], jnp.concatenate(wide, axis=0), load_staged_rhs=0 if n // batch < 2 else None)
        linear = pltpu.matmul_pop(products[q])[:, :features] + bias
        result = (jnp.concatenate(bases, axis=0) + jnp.maximum(linear, 0.0)).astype(jnp.bfloat16)
        out_ref[n * per_row : (n + batch) * per_row] = result.reshape(batch * per_row, dst, features)


def swap(x, group, m):
    return lax.ppermute(x, "feat", [(i, i ^ m) for i in range(group)])


def per_device(feats, weight, bias, neighbours, counts, adj_words, tile_row):
    group, bands = lax.axis_size("feat"), lax.axis_size("tiles")
    me = lax.axis_index("feat")
    tiles, dst, features = feats.shape
    _, slots, words, cells = adj_words.shape
    half = tiles // 2
    per_row = LANES // dst
    rows = tiles // per_row
    assert half >= REACH and rows % 4 == 0 and per_row % 2 == 0 and bands % 2 == 0 and features == LANES
    sizes = [rows // 2, rows - rows // 2]

    shapes = [jax.ShapeDtypeStruct((n, slots, words, LANES), jnp.int16) for n in sizes for _ in range(group)]
    block = min(sizes) * per_row
    packed = pl.pallas_call(
        lambda *refs: pack_kernel(group, dst, per_row, BITS - (words * BITS - cells), sizes, *refs),
        out_shape=shapes,
        grid=(tiles // block,),
        in_specs=[SMEM, pl.BlockSpec((block, slots, words, cells), lambda i: (i, 0, 0, 0))],
        out_specs=[pl.BlockSpec(s.shape, lambda i: (0, 0, 0, 0)) for s in shapes],
        cost_estimate=pl.CostEstimate(flops=3 * 10**9, bytes_accessed=5 * 10**6, transcendentals=0),
        name="pack",
    )(counts, adj_words)

    direct = [1 << n for n in range(group.bit_length() - 1)]
    far = [m for m in range(group) if m & (m - 1)]
    near = [feats] + [swap(feats, group, m) for m in direct]
    weight_pieces = [weight] + [swap(weight, group, m) for m in range(1, group)]
    inner_bits = list(range(1, len(direct)))
    outer_bits = list(range(2, len(direct) + 1))
    together = jax.ShapeDtypeStruct((len(near), half, dst, features), jnp.bfloat16)
    alone = jax.ShapeDtypeStruct((half, dst, features), jnp.bfloat16)
    inner, *rest = pl.pallas_call(
        lambda *refs: arrange_kernel(len(near), inner_bits, outer_bits, *refs),
        out_shape=[together] + [alone] * len(inner_bits) + [together] + [alone] * len(outer_bits),
        in_specs=[SMEM] + [VMEM] * len(near),
        out_specs=[VMEM] * (2 + len(inner_bits) + len(outer_bits)),
        compiler_params=pltpu.CompilerParams(vmem_limit_bytes=4 * 2**20),
        cost_estimate=pl.CostEstimate(flops=10**9, bytes_accessed=10**6, transcendentals=0),
        name="arrange",
    )(tile_row, *near)
    inners = {direct[n - 1]: part for n, part in zip(inner_bits, rest)}
    outer, *rest = rest[len(inner_bits) :]
    outers = {direct[n - 1]: part for n, part in zip(outer_bits, rest)}
    for m in far:
        bits = [bit for bit in direct if m & bit]
        inners[m] = swap(inners[m ^ bits[-1]], group, bits[-1])
        outers[m] = swap(outers[m ^ bits[0]], group, bits[0])
    inners, outers = [inner] + [inners[m] for m in far], [outer] + [outers[m] for m in far]
    exchanged = []
    for c in range(len(sizes)):
        parts = packed[c * group : (c + 1) * group]
        exchanged += [parts[0]] + [swap(parts[m], group, m) for m in range(1, group)]

    inside = [(i, i ^ 1) for i in range(bands)]
    across = [pair for i in range(1, bands - 1, 2) for pair in ((i, i + 1), (i + 1, i))]
    from_inside, from_across = [], []
    for n in range(len(inners)):
        from_across.append(lax.ppermute(outers[n], "tiles", across))
        from_inside.append(lax.ppermute(inners[n], "tiles", inside))

    cell = row_cells(words, cells)
    column = ((cell // dst) ^ me) * dst + cell % dst
    perm = (column[:, None] == jnp.arange(cells, dtype=jnp.int32)[None, :]).astype(jnp.bfloat16)
    reachable_shape = jax.ShapeDtypeStruct((4 * half, cells, features), jnp.bfloat16)
    assemble = functools.partial(
        pl.pallas_call,
        compiler_params=pltpu.CompilerParams(vmem_limit_bytes=4 * 2**20),
        cost_estimate=pl.CostEstimate(flops=2 * 10**9, bytes_accessed=4 * 10**6, transcendentals=0),
        name="assemble",
    )
    sides = inners + outers + weight_pieces
    reachable, weight_wide = assemble(
        lambda *refs: assemble_kernel(group, ((2, 1), (1, 2)), *refs),
        out_shape=[reachable_shape, jax.ShapeDtypeStruct((2 * features, 2 * features), jnp.bfloat16)],
        in_specs=[VMEM] * (1 + len(sides)),
        out_specs=[VMEM] * 2,
    )(perm, *sides)
    sides = from_inside + from_across
    reachable = assemble(
        lambda *refs: assemble_kernel(group, ((3, 0), (0, 3)), *refs),
        out_shape=reachable_shape,
        in_specs=[VMEM] * (2 + len(sides)),
        out_specs=VMEM,
        input_output_aliases={1 + len(sides): 0},
    )(perm, *sides, reachable)

    return pl.pallas_call(
        lambda *refs: main_kernel(group, dst, per_row, *refs),
        out_shape=jax.ShapeDtypeStruct(feats.shape, feats.dtype),
        in_specs=[SMEM] + [VMEM] * (4 + len(exchanged)),
        out_specs=VMEM,
        scratch_shapes=[
            pltpu.VMEM((rows + 1, LANES, features), jnp.float32),
            pltpu.VMEM((rows + 1, SUB, LANES), jnp.float32),
        ],
        compiler_params=pltpu.CompilerParams(vmem_limit_bytes=12 * 2**20),
        cost_estimate=pl.CostEstimate(flops=10**10, bytes_accessed=10**7, transcendentals=0),
        name="main",
    )(neighbours.T, reachable, weight_wide, bias[None, :], feats, *exchanged)


def solution(mesh):
    return jax.shard_map(
        per_device,
        mesh=mesh,
        in_specs=(
            P("tiles", "feat", None),
            P("feat", None),
            P(),
            P("tiles", None),
            P("tiles"),
            P("tiles", "feat", None, None),
            P(),
        ),
        out_specs=P("tiles", "feat", None),
        check_vma=False,
    )
```

time: 75.2 us -> 73 us (0.971)
  the two profiles are of different devices: /device:TPU:0 before, /device:TPU:12 now
where the time goes in v1:
time: 73 us; the launch traced here: 72.8 us
  waiting for transfers between devices  36 us (49%)
  Pallas kernels  17.9 us (25%)
  starting transfers between devices  16.9 us (23%)
  local copies, waits for them, and re-layouts  1.76 us (2%)
    ppermute x13, waiting for transfers between devices, swap(): return lax.ppermute(x, 'feat', [(i, i ^ m) for i in range(group)])  36 us
    ppermute x13, starting transfers between devices, swap(): return lax.ppermute(x, 'feat', [(i, i ^ m) for i in range(group)])  12.6 us
    pallas_call x1, Pallas kernels, per_device(): pl.pallas_call(lambda *refs: main_kernel(group, dst, per_row, *refs), out...  8.96 us
    ppermute x2, starting transfers between devices, per_device(): from_across.append(lax.ppermute(outers[n], 'tiles', across))  4.37 us
    pallas_call x1, Pallas kernels, per_device(): pl.pallas_call(lambda *refs: pack_kernel(group, dst, per_row, BITS - (wor...  3.9 us
    pallas_call x1, Pallas kernels, per_device(): assemble(lambda *refs: assemble_kernel(group, ((2, 1), (1, 2)), *refs), o...  2.2 us
    unnamed x20, local copies, waits for them, and re-layouts  1.76 us
    pallas_call x1, Pallas kernels, per_device(): pl.pallas_call(lambda *refs: arrange_kernel(len(near), inner_bits, outer_...  1.56 us
  transfers between devices with their start and end apart: 17, of which 9 were waited for; matrix products, arithmetic and copies ran while one was open for 0% of the time, Pallas kernels for 10%

profile of v1, /device:TPU:12, one launch (start us, length us, event | category | flops | bytes accessed | tf_op | source)
XLA Modules:
  0.0 72.8 jit_solution(17519445357779878267)
XLA Ops:
  0.0 1.5 %collective-permute-start = (bf16[32,64,128]{2,1,0:T(8,128)(2,1)}, bf16[32,64,128]{2,1,0:T(8,128)(2,1)S(1)}, u32[]{:S(2)}, u32[]{:S(2)}) collective-permute-start(bf16[32,64,128]{2,1,0:T(8,128)(2,1)} %refs_4_.1), channel_id=1, source_target_pairs={{0,1},{1,0},{2,3},{3,2},{4,5},{5,4},{6,7},{7,6},{8,9},{9,8},{10,11... | collective-permute-start | bytes 1572872 | tf_op jit(solution)/shard_map/ppermute | solution.py:229
  1.5 0.5 collective-permute-start.1
  2.0 11.9 %collective-permute-done.refs_2_ = bf16[32,64,128]{2,1,0:T(8,128)(2,1)S(1)} collective-permute-done((bf16[32,64,128]{2,1,0:T(8,128)(2,1)}, bf16[32,64,128]{2,1,0:T(8,128)(2,1)S(1)}, u32[]{:S(2)}, u32[]{:S(2)}) %collective-permute-start) | collective-permute-done | bytes 524320 | tf_op jit(solution)/shard_map/ppermute | solution.py:229
  13.9 1.2 %collective-permute-done.1.refs_3_ = bf16[32,64,128]{2,1,0:T(8,128)(2,1)S(1)} collective-permute-done((bf16[32,64,128]{2,1,0:T(8,128)(2,1)}, bf16[32,64,128]{2,1,0:T(8,128)(2,1)S(1)}, u32[]{:S(2)}, u32[]{:S(2)}) %collective-permute-start.1) | collective-permute-done | bytes 524320 | tf_op jit(solution)/shard_map/ppermute | solution.py:229
  15.1 1.0 %copy-done = bf16[32,64,128]{2,1,0:T(8,128)(2,1)S(1)} copy-done((bf16[32,64,128]{2,1,0:T(8,128)(2,1)S(1)}, bf16[32,64,128]{2,1,0:T(8,128)(2,1)}, u32[]{:S(2)}) %copy-start) | copy-done | bytes 524312
  16.1 0.7 copy-done.4
  16.8 1.6 %arrange.1 = (bf16[3,16,64,128]{3,2,1,0:T(8,128)(2,1)S(1)}, bf16[16,64,128]{2,1,0:T(8,128)(2,1)}, bf16[3,16,64,128]{3,2,1,0:T(8,128)(2,1)S(1)}, bf16[16,64,128]{2,1,0:T(8,128)(2,1)}) custom-call(s32[256]{0:T(256)S(1)} %copy-done.4, bf16[32,64,128]{2,1,0:T(8,128)(2,1)S(1)} %copy-done, bf16[32,64,128]{2,1,0:T(8,128)(2,1)S(1)} %collective-permute-done.refs_2_, ...), custom_call_target="tpu_custom_call" | custom-call | flops 1000000000 | bytes 1000000 | tf_op jit(solution)/shard_map/arrange/pallas_call | solution.py:263
  18.4 2.5 %collective-permute-start.5 = (bf16[3,16,64,128]{3,2,1,0:T(8,128)(2,1)S(1)}, bf16[3,16,64,128]{3,2,1,0:T(8,128)(2,1)S(1)}, u32[]{:S(2)}, u32[]{:S(2)}) collective-permute-start(bf16[3,16,64,128]{3,2,1,0:T(8,128)(2,1)S(1)} %get-tuple-element.21.refs_3_), channel_id=1, source_target_pairs={{4,8},{8,4},{12,16},{16,12},{20,24},{24,20},{5,9},{9,5},{13,17},{1... | collective-permute-start | bytes 2359304 | tf_op jit(solution)/shard_map/ppermute | solution.py:289
  20.8 0.4 collective-permute-start.10
  21.2 1.7 %collective-permute-start.8 = (bf16[32,128]{1,0:T(8,128)(2,1)}, bf16[32,128]{1,0:T(8,128)(2,1)S(1)}, u32[]{:S(2)}, u32[]{:S(2)}) collective-permute-start(bf16[32,128]{1,0:T(8,128)(2,1)} %refs_5_.1), channel_id=1, source_target_pairs={{0,1},{1,0},{2,3},{3,2},{4,5},{5,4},{6,7},{7,6},{8,9},{9,8},{10,11... | collective-permute-start | bytes 24584 | tf_op jit(solution)/shard_map/ppermute | solution.py:229
  22.9 1.5 %collective-permute-start.3 = (bf16[16,64,128]{2,1,0:T(8,128)(2,1)}, bf16[16,64,128]{2,1,0:T(8,128)(2,1)S(1)}, u32[]{:S(2)}, u32[]{:S(2)}) collective-permute-start(bf16[16,64,128]{2,1,0:T(8,128)(2,1)} %get-tuple-element.20), channel_id=1, source_target_pairs={{0,2},{1,3},{2,0},{3,1},{4,6},{5,7},{6,4},{7,5},{8,10},{9,11},{10,... | collective-permute-start | bytes 786440 | tf_op jit(solution)/shard_map/ppermute | solution.py:229
  24.4 1.3 %collective-permute-done.10.refs_8_ = bf16[32,128]{1,0:T(8,128)(2,1)S(1)} collective-permute-done((bf16[32,128]{1,0:T(8,128)(2,1)}, bf16[32,128]{1,0:T(8,128)(2,1)S(1)}, u32[]{:S(2)}, u32[]{:S(2)}) %collective-permute-start.10) | collective-permute-done | bytes 8224 | tf_op jit(solution)/shard_map/ppermute | solution.py:229
  25.7 0.5 collective-permute-start.6
  26.2 3.9 %pack.1 = (s16[8,4,24,128]{3,2,1,0:T(8,128)(2,1)}, s16[8,4,24,128]{3,2,1,0:T(8,128)(2,1)}, s16[8,4,24,128]{3,2,1,0:T(8,128)(2,1)}, s16[8,4,24,128]{3,2,1,0:T(8,1...) custom-call(s32[32]{0:T(128)} %refs_0_.3, ...), custom_call_target="tpu_custom_call" | custom-call | flops 3000000000 | bytes 5000000 | tf_op jit(solution)/shard_map/pack/pallas_call | solution.py:245
  30.1 0.4 collective-permute-start.9
  30.5 1.4 %collective-permute-done.3.refs_2_ = bf16[16,64,128]{2,1,0:T(8,128)(2,1)S(1)} collective-permute-done((bf16[16,64,128]{2,1,0:T(8,128)(2,1)}, bf16[16,64,128]{2,1,0:T(8,128)(2,1)S(1)}, u32[]{:S(2)}, u32[]{:S(2)}) %collective-permute-start.3) | collective-permute-done | bytes 262176 | tf_op jit(solution)/shard_map/ppermute | solution.py:229
  31.9 2.4 %collective-permute-done.6.refs_4_ = bf16[16,64,128]{2,1,0:T(8,128)(2,1)} collective-permute-done((bf16[16,64,128]{2,1,0:T(8,128)(2,1)}, bf16[16,64,128]{2,1,0:T(8,128)(2,1)}, u32[]{:S(2)}, u32[]{:S(2)}) %collective-permute-start.6) | collective-permute-done | bytes 262176 | tf_op jit(solution)/shard_map/ppermute | solution.py:229
  34.3 1.9 %collective-permute-start.7 = (bf16[16,64,128]{2,1,0:T(8,128)(2,1)}, bf16[16,64,128]{2,1,0:T(8,128)(2,1)S(1)}, u32[]{:S(2)}, u32[]{:S(2)}) collective-permute-start(bf16[16,64,128]{2,1,0:T(8,128)(2,1)} %collective-permute-done.6.refs_4_), channel_id=1, source_target_pairs={{4,8},{8,4},{12,16},{16,12},{20,24},{24,20},{5,9},{9,5},{13,17},{1... | collective-permute-start | bytes 786440 | tf_op jit(solution)/shard_map/ppermute | solution.py:289
  36.3 0.6 collective-permute-start.11
  36.9 0.1 fusion.refs_0_
  37.0 6.6 %collective-permute-done.11.refs_6_ = s16[8,4,24,128]{3,2,1,0:T(8,128)(2,1)S(1)} collective-permute-done((s16[8,4,24,128]{3,2,1,0:T(8,128)(2,1)}, s16[8,4,24,128]{3,2,1,0:T(8,128)(2,1)S(1)}, u32[]{:S(2)}, u32[]{:S(2)}) %collective-permute-start.11) | collective-permute-done | bytes 196640 | tf_op jit(solution)/shard_map/ppermute | solution.py:229
  43.6 0.5 collective-permute-start.12
  44.1 1.5 %collective-permute-start.13 = (s16[8,4,24,128]{3,2,1,0:T(8,128)(2,1)}, s16[8,4,24,128]{3,2,1,0:T(8,128)(2,1)S(1)}, u32[]{:S(2)}, u32[]{:S(2)}) collective-permute-start(s16[8,4,24,128]{3,2,1,0:T(8,128)(2,1)} %get-tuple-element.28), channel_id=1, source_target_pairs={{0,3},{1,2},{2,1},{3,0},{4,7},{5,6},{6,5},{7,4},{8,11},{9,10},{10,... | collective-permute-start | bytes 589832 | tf_op jit(solution)/shard_map/ppermute | solution.py:229
  45.6 1.5 %collective-permute-start.14 = (s16[8,4,24,128]{3,2,1,0:T(8,128)(2,1)}, s16[8,4,24,128]{3,2,1,0:T(8,128)(2,1)S(1)}, u32[]{:S(2)}, u32[]{:S(2)}) collective-permute-start(s16[8,4,24,128]{3,2,1,0:T(8,128)(2,1)} %get-tuple-element.30), channel_id=1, source_target_pairs={{0,1},{1,0},{2,3},{3,2},{4,5},{5,4},{6,7},{7,6},{8,9},{9,8},{10,11... | collective-permute-start | bytes 589832 | tf_op jit(solution)/shard_map/ppermute | solution.py:229
  47.1 0.5 collective-permute-start.15
  47.6 1.5 %collective-permute-start.16 = (s16[8,4,24,128]{3,2,1,0:T(8,128)(2,1)}, s16[8,4,24,128]{3,2,1,0:T(8,128)(2,1)S(1)}, u32[]{:S(2)}, u32[]{:S(2)}) collective-permute-start(s16[8,4,24,128]{3,2,1,0:T(8,128)(2,1)} %get-tuple-element.32), channel_id=1, source_target_pairs={{0,3},{1,2},{2,1},{3,0},{4,7},{5,6},{6,5},{7,4},{8,11},{9,10},{10,... | collective-permute-start | bytes 589832 | tf_op jit(solution)/shard_map/ppermute | solution.py:229
  49.1 2.2 %assemble.2 = (bf16[64,256,128]{2,1,0:T(8,128)(2,1)S(1)}, bf16[256,256]{1,0:T(8,128)(2,1)S(1)}) custom-call(bf16[256,256]{1,0:T(8,128)(2,1)S(1)} %fusion.refs_0_, bf16[3,16,64,128]{3,2,1,0:T(8,128)(2,1)S(1)} %get-tuple-element.19.refs_1_, bf16[16,64,128]{2,1,0:T(8,128)(2,1)S(1)} %collective-permute-done.3.refs_2_, ...), custom_call_target="tpu_custom_call" | custom-call | flops 2000000000 | bytes 4000000 | tf_op jit(solution)/shard_map/assemble/pallas_call | solution.py:303
  51.4 1.2 %assemble.3.refs_1_ = bf16[64,256,128]{2,1,0:T(8,128)(2,1)S(1)} custom-call(bf16[256,256]{1,0:T(8,128)(2,1)S(1)} %fusion.refs_0_, bf16[3,16,64,128]{3,2,1,0:T(8,128)(2,1)S(1)} %collective-permute-done.2.refs_1_, bf16[16,64,128]{2,1,0:T(8,128)(2,1)S(1)} %collective-permute-done.4.refs_2_, ...), custom_call_target="tpu_custom_call", output_to_operand_aliasing={{}: (5, {})} | custom-call | flops 2000000000 | bytes 4000000 | tf_op jit(solution)/shard_map/assemble/pallas_call | solution.py:310
  52.6 3.2 %collective-permute-done.12.refs_7_ = s16[8,4,24,128]{3,2,1,0:T(8,128)(2,1)S(1)} collective-permute-done((s16[8,4,24,128]{3,2,1,0:T(8,128)(2,1)}, s16[8,4,24,128]{3,2,1,0:T(8,128)(2,1)S(1)}, u32[]{:S(2)}, u32[]{:S(2)}) %collective-permute-start.12) | collective-permute-done | bytes 196640 | tf_op jit(solution)/shard_map/ppermute | solution.py:229
  55.8 1.5 %collective-permute-done.14.refs_10_ = s16[8,4,24,128]{3,2,1,0:T(8,128)(2,1)S(1)} collective-permute-done((s16[8,4,24,128]{3,2,1,0:T(8,128)(2,1)}, s16[8,4,24,128]{3,2,1,0:T(8,128)(2,1)S(1)}, u32[]{:S(2)}, u32[]{:S(2)}) %collective-permute-start.14) | collective-permute-done | bytes 196640 | tf_op jit(solution)/shard_map/ppermute | solution.py:229
  57.3 6.5 %collective-permute-done.15.refs_11_ = s16[8,4,24,128]{3,2,1,0:T(8,128)(2,1)S(1)} collective-permute-done((s16[8,4,24,128]{3,2,1,0:T(8,128)(2,1)}, s16[8,4,24,128]{3,2,1,0:T(8,128)(2,1)S(1)}, u32[]{:S(2)}, u32[]{:S(2)}) %collective-permute-start.15) | collective-permute-done | bytes 196640 | tf_op jit(solution)/shard_map/ppermute | solution.py:229
  63.8 9.0 %main.1 = bf16[32,64,128]{2,1,0:T(8,128)(2,1)} custom-call(s32[16,32]{1,0:T(8,128)S(1)} %bitcast.2, bf16[64,256,128]{2,1,0:T(8,128)(2,1)S(1)} %assemble.3.refs_1_, bf16[256,256]{1,0:T(8,128)(2,1)S(1)} %get-tuple-element.24.refs_2_, f32[1,128]{1,0:T(1,128)S(1)} %bitcast.3, bf16[32,64,128]{2,1,0:T(8,128)(2,1)S(1)} %copy-done.1, ...), custom_call_target="tpu_custom_call" | custom-call | flops 10000000000 | bytes 10000000 | tf_op jit(solution)/shard_map/main/pallas_call | solution.py:318
  (29 shorter events, 0.1 us)
Async XLA Ops:
  0.0 13.9 %collective-permute-start = (bf16[32,64,128]{2,1,0:T(8,128)(2,1)}, bf16[32,64,128]{2,1,0:T(8,128)(2,1)S(1)}, u32[]{:S(2)}, u32[]{:S(2)}) collective-permute-start(bf16[32,64,128]{2,1,0:T(8,128)(2,1)} %refs_4_.1), channel_id=1, source_target_pairs={{0,1},{1,0},{2,3},{3,2},{4,5},{5,4},{6,7},{7,6},{8,9},{9,8},{10,11... | collective-permute-start | bytes 1572872 | tf_op jit(solution)/shard_map/ppermute | solution.py:229
  1.5 13.6 %collective-permute-start.1 = (bf16[32,64,128]{2,1,0:T(8,128)(2,1)}, bf16[32,64,128]{2,1,0:T(8,128)(2,1)S(1)}, u32[]{:S(2)}, u32[]{:S(2)}) collective-permute-start(bf16[32,64,128]{2,1,0:T(8,128)(2,1)} %refs_4_.1), channel_id=1, source_target_pairs={{0,2},{1,3},{2,0},{3,1},{4,6},{5,7},{6,4},{7,5},{8,10},{9,11},{10,... | collective-permute-start | bytes 1572872 | tf_op jit(solution)/shard_map/ppermute | solution.py:229
  15.1 1.0 %copy-start = (bf16[32,64,128]{2,1,0:T(8,128)(2,1)S(1)}, bf16[32,64,128]{2,1,0:T(8,128)(2,1)}, u32[]{:S(2)}) copy-start(bf16[32,64,128]{2,1,0:T(8,128)(2,1)} %refs_4_.1) | copy-start | bytes 1572868
  16.1 0.7 copy-start.4
  18.4 28.7 %collective-permute-start.2 = (bf16[3,16,64,128]{3,2,1,0:T(8,128)(2,1)S(1)}, bf16[3,16,64,128]{3,2,1,0:T(8,128)(2,1)S(1)}, u32[]{:S(2)}, u32[]{:S(2)}) collective-permute-start(bf16[3,16,64,128]{3,2,1,0:T(8,128)(2,1)S(1)} %get-tuple-element.19.refs_1_), channel_id=1, source_target_pairs={{0,4},{4,0},{8,12},{12,8},{16,20},{20,16},{24,28},{28,24},{1,5},{5... | collective-permute-start | bytes 2359304 | tf_op jit(solution)/shard_map/ppermute | solution.py:290
  18.4 29.3 %collective-permute-start.5 = (bf16[3,16,64,128]{3,2,1,0:T(8,128)(2,1)S(1)}, bf16[3,16,64,128]{3,2,1,0:T(8,128)(2,1)S(1)}, u32[]{:S(2)}, u32[]{:S(2)}) collective-permute-start(bf16[3,16,64,128]{3,2,1,0:T(8,128)(2,1)S(1)} %get-tuple-element.21.refs_3_), channel_id=1, source_target_pairs={{4,8},{8,4},{12,16},{16,12},{20,24},{24,20},{5,9},{9,5},{13,17},{1... | collective-permute-start | bytes 2359304 | tf_op jit(solution)/shard_map/ppermute | solution.py:289
  20.8 4.8 %collective-permute-start.10 = (bf16[32,128]{1,0:T(8,128)(2,1)}, bf16[32,128]{1,0:T(8,128)(2,1)S(1)}, u32[]{:S(2)}, u32[]{:S(2)}) collective-permute-start(bf16[32,128]{1,0:T(8,128)(2,1)} %refs_5_.1), channel_id=1, source_target_pairs={{0,3},{1,2},{2,1},{3,0},{4,7},{5,6},{6,5},{7,4},{8,11},{9,10},{10,... | collective-permute-start | bytes 24584 | tf_op jit(solution)/shard_map/ppermute | solution.py:229
  21.2 8.9 %collective-permute-start.8 = (bf16[32,128]{1,0:T(8,128)(2,1)}, bf16[32,128]{1,0:T(8,128)(2,1)S(1)}, u32[]{:S(2)}, u32[]{:S(2)}) collective-permute-start(bf16[32,128]{1,0:T(8,128)(2,1)} %refs_5_.1), channel_id=1, source_target_pairs={{0,1},{1,0},{2,3},{3,2},{4,5},{5,4},{6,7},{7,6},{8,9},{9,8},{10,11... | collective-permute-start | bytes 24584 | tf_op jit(solution)/shard_map/ppermute | solution.py:229
  22.9 9.0 %collective-permute-start.3 = (bf16[16,64,128]{2,1,0:T(8,128)(2,1)}, bf16[16,64,128]{2,1,0:T(8,128)(2,1)S(1)}, u32[]{:S(2)}, u32[]{:S(2)}) collective-permute-start(bf16[16,64,128]{2,1,0:T(8,128)(2,1)} %get-tuple-element.20), channel_id=1, source_target_pairs={{0,2},{1,3},{2,0},{3,1},{4,6},{5,7},{6,4},{7,5},{8,10},{9,11},{10,... | collective-permute-start | bytes 786440 | tf_op jit(solution)/shard_map/ppermute | solution.py:229
  25.7 4.5 %copy-start.2 = (bf16[32,128]{1,0:T(8,128)(2,1)S(1)}, bf16[32,128]{1,0:T(8,128)(2,1)}, u32[]{:S(2)}) copy-start(bf16[32,128]{1,0:T(8,128)(2,1)} %refs_5_.1) | copy-start | bytes 24580
  25.7 10.6 %copy-start.8 = (s32[256]{0:T(256)S(1)}, s32[256]{0:T(256)}, u32[]{:S(2)}) copy-start(s32[256]{0:T(256)} %constant.10.clone) | copy-start | bytes 3076
  25.7 10.6 %copy-start.9 = (s32[256]{0:T(256)S(1)}, s32[256]{0:T(256)}, u32[]{:S(2)}) copy-start(s32[256]{0:T(256)} %constant.11.clone) | copy-start | bytes 3076
  25.7 8.6 %collective-permute-start.6 = (bf16[16,64,128]{2,1,0:T(8,128)(2,1)}, bf16[16,64,128]{2,1,0:T(8,128)(2,1)}, u32[]{:S(2)}, u32[]{:S(2)}) collective-permute-start(bf16[16,64,128]{2,1,0:T(8,128)(2,1)} %get-tuple-element.22), channel_id=1, source_target_pairs={{0,1},{1,0},{2,3},{3,2},{4,5},{5,4},{6,7},{7,6},{8,9},{9,8},{10,11... | collective-permute-start | bytes 786440 | tf_op jit(solution)/shard_map/ppermute | solution.py:229
  30.1 6.1 %collective-permute-start.9 = (bf16[32,128]{1,0:T(8,128)(2,1)S(1)}, bf16[32,128]{1,0:T(8,128)(2,1)S(1)}, u32[]{:S(2)}, u32[]{:S(2)}) collective-permute-start(bf16[32,128]{1,0:T(8,128)(2,1)S(1)} %copy-done.2), channel_id=1, source_target_pairs={{0,2},{1,3},{2,0},{3,1},{4,6},{5,7},{6,4},{7,5},{8,10},{9,11},{10,... | collective-permute-start | bytes 24584 | tf_op jit(solution)/shard_map/ppermute | solution.py:229
  31.9 12.3 %collective-permute-start.4 = (bf16[16,64,128]{2,1,0:T(8,128)(2,1)S(1)}, bf16[16,64,128]{2,1,0:T(8,128)(2,1)S(1)}, u32[]{:S(2)}, u32[]{:S(2)}) collective-permute-start(bf16[16,64,128]{2,1,0:T(8,128)(2,1)S(1)} %collective-permute-done.3.refs_2_), channel_id=1, source_target_pairs={{0,4},{4,0},{8,12},{12,8},{16,20},{20,16},{24,28},{28,24},{1,5},{5... | collective-permute-start | bytes 786440 | tf_op jit(solution)/shard_map/ppermute | solution.py:290
  34.3 11.3 %collective-permute-start.7 = (bf16[16,64,128]{2,1,0:T(8,128)(2,1)}, bf16[16,64,128]{2,1,0:T(8,128)(2,1)S(1)}, u32[]{:S(2)}, u32[]{:S(2)}) collective-permute-start(bf16[16,64,128]{2,1,0:T(8,128)(2,1)} %collective-permute-done.6.refs_4_), channel_id=1, source_target_pairs={{4,8},{8,4},{12,16},{16,12},{20,24},{24,20},{5,9},{9,5},{13,17},{1... | collective-permute-start | bytes 786440 | tf_op jit(solution)/shard_map/ppermute | solution.py:289
  36.3 7.3 %collective-permute-start.11 = (s16[8,4,24,128]{3,2,1,0:T(8,128)(2,1)}, s16[8,4,24,128]{3,2,1,0:T(8,128)(2,1)S(1)}, u32[]{:S(2)}, u32[]{:S(2)}) collective-permute-start(s16[8,4,24,128]{3,2,1,0:T(8,128)(2,1)} %get-tuple-element.26), channel_id=1, source_target_pairs={{0,1},{1,0},{2,3},{3,2},{4,5},{5,4},{6,7},{7,6},{8,9},{9,8},{10,11... | collective-permute-start | bytes 589832 | tf_op jit(solution)/shard_map/ppermute | solution.py:229
  43.6 12.2 %collective-permute-start.12 = (s16[8,4,24,128]{3,2,1,0:T(8,128)(2,1)}, s16[8,4,24,128]{3,2,1,0:T(8,128)(2,1)S(1)}, u32[]{:S(2)}, u32[]{:S(2)}) collective-permute-start(s16[8,4,24,128]{3,2,1,0:T(8,128)(2,1)} %get-tuple-element.27), channel_id=1, source_target_pairs={{0,2},{1,3},{2,0},{3,1},{4,6},{5,7},{6,4},{7,5},{8,10},{9,11},{10,... | collective-permute-start | bytes 589832 | tf_op jit(solution)/shard_map/ppermute | solution.py:229
  44.1 11.7 %collective-permute-start.13 = (s16[8,4,24,128]{3,2,1,0:T(8,128)(2,1)}, s16[8,4,24,128]{3,2,1,0:T(8,128)(2,1)S(1)}, u32[]{:S(2)}, u32[]{:S(2)}) collective-permute-start(s16[8,4,24,128]{3,2,1,0:T(8,128)(2,1)} %get-tuple-element.28), channel_id=1, source_target_pairs={{0,3},{1,2},{2,1},{3,0},{4,7},{5,6},{6,5},{7,4},{8,11},{9,10},{10,... | collective-permute-start | bytes 589832 | tf_op jit(solution)/shard_map/ppermute | solution.py:229
  45.6 11.7 %collective-permute-start.14 = (s16[8,4,24,128]{3,2,1,0:T(8,128)(2,1)}, s16[8,4,24,128]{3,2,1,0:T(8,128)(2,1)S(1)}, u32[]{:S(2)}, u32[]{:S(2)}) collective-permute-start(s16[8,4,24,128]{3,2,1,0:T(8,128)(2,1)} %get-tuple-element.30), channel_id=1, source_target_pairs={{0,1},{1,0},{2,3},{3,2},{4,5},{5,4},{6,7},{7,6},{8,9},{9,8},{10,11... | collective-permute-start | bytes 589832 | tf_op jit(solution)/shard_map/ppermute | solution.py:229
  47.1 16.7 %collective-permute-start.15 = (s16[8,4,24,128]{3,2,1,0:T(8,128)(2,1)}, s16[8,4,24,128]{3,2,1,0:T(8,128)(2,1)S(1)}, u32[]{:S(2)}, u32[]{:S(2)}) collective-permute-start(s16[8,4,24,128]{3,2,1,0:T(8,128)(2,1)} %get-tuple-element.31), channel_id=1, source_target_pairs={{0,2},{1,3},{2,0},{3,1},{4,6},{5,7},{6,4},{7,5},{8,10},{9,11},{10,... | collective-permute-start | bytes 589832 | tf_op jit(solution)/shard_map/ppermute | solution.py:229
  47.6 16.2 %collective-permute-start.16 = (s16[8,4,24,128]{3,2,1,0:T(8,128)(2,1)}, s16[8,4,24,128]{3,2,1,0:T(8,128)(2,1)S(1)}, u32[]{:S(2)}, u32[]{:S(2)}) collective-permute-start(s16[8,4,24,128]{3,2,1,0:T(8,128)(2,1)} %get-tuple-element.32), channel_id=1, source_target_pairs={{0,3},{1,2},{2,1},{3,0},{4,7},{5,6},{6,5},{7,4},{8,11},{9,10},{10,... | collective-permute-start | bytes 589832 | tf_op jit(solution)/shard_map/ppermute | solution.py:229
  51.3 12.5 %copy-start.1 = (bf16[32,64,128]{2,1,0:T(8,128)(2,1)S(1)}, bf16[32,64,128]{2,1,0:T(8,128)(2,1)}, u32[]{:S(2)}) copy-start(bf16[32,64,128]{2,1,0:T(8,128)(2,1)} %refs_4_.1) | copy-start | bytes 1572868
  51.3 12.5 %copy-start.3 = (s32[32,16]{0,1:T(8,128)S(1)}, s32[32,16]{0,1:T(8,128)}, u32[]{:S(2)}) copy-start(s32[32,16]{0,1:T(8,128)} %param.12) | copy-start | bytes 6148
  51.3 12.5 %copy-start.5 = (f32[128]{0:T(128)S(1)}, f32[128]{0:T(128)}, u32[]{:S(2)}) copy-start(f32[128]{0:T(128)} %param.11) | copy-start | bytes 1540
  51.4 12.5 %copy-start.6 = (s16[8,4,24,128]{3,2,1,0:T(8,128)(2,1)S(1)}, s16[8,4,24,128]{3,2,1,0:T(8,128)(2,1)}, u32[]{:S(2)}) copy-start(s16[8,4,24,128]{3,2,1,0:T(8,128)(2,1)} %get-tuple-element.25.refs_5_) | copy-start | bytes 589828
  51.4 12.5 %copy-start.7 = (s16[8,4,24,128]{3,2,1,0:T(8,128)(2,1)S(1)}, s16[8,4,24,128]{3,2,1,0:T(8,128)(2,1)}, u32[]{:S(2)}) copy-start(s16[8,4,24,128]{3,2,1,0:T(8,128)(2,1)} %get-tuple-element.29.refs_9_) | copy-start | bytes 589828

commit v2 on v1

--- a/solution.py
+++ b/solution.py
@@ -1,4 +1,5 @@
 import functools
+import math
 
 import jax
 import jax.numpy as jnp
@@ -96,64 +97,65 @@
                     alone[n][i] = tile
 
 
-def assemble_kernel(group, places, perm_ref, *refs):
+def split(group):
+    near = [0] + [1 << n for n in range(group.bit_length() - 1)]
+    return near, [m for m in range(group) if m not in near]
+
+
+def tile_of(group, side, tile):
+    near, far = split(group)
+    cut = {m: side[0][n, tile] for n, m in enumerate(near)} | {m: side[1 + n][tile] for n, m in enumerate(far)}
+    return jnp.concatenate([cut[m] for m in range(group)], axis=0)
+
+
+def assemble_kernel(group, perm_ref, *refs):
+    *pieces, tiles_ref, weight_ref = refs
     perm = perm_ref[...]
     odd = lax.axis_index("tiles") % 2
-    near = [0] + [1 << n for n in range(group.bit_length() - 1)]
-    far = [m for m in range(group) if m not in near]
-    per_side = 1 + len(far)
-    tiles_ref = refs[2 * per_side + group] if len(refs) > 2 * per_side + group else refs[-1]
+    per_side = (len(pieces) - group) // 2
 
     def step(base, side, i, carry):
-        pair = []
-        for j in range(2):
-            tile = 2 * i + j
-            cut = {m: side[0][n, tile] for n, m in enumerate(near)} | {m: side[1 + n][tile] for n, m in enumerate(far)}
-            pair.append(jnp.concatenate([cut[m] for m in range(group)], axis=0))
+        pair = [tile_of(group, side, 2 * i + j) for j in range(2)]
         got = jnp.dot(perm, jnp.concatenate(pair, axis=1), preferred_element_type=jnp.float32)
         for j in range(2):
             tiles_ref[base + 2 * i + j] = got[:, j * LANES : (j + 1) * LANES].astype(jnp.bfloat16)
         return carry
 
-    for n, (even_place, odd_place) in enumerate(places):
-        side = refs[n * per_side : (n + 1) * per_side]
+    for n in range(2):
+        side = pieces[n * per_side : (n + 1) * per_side]
         half = side[0].shape[1]
-        base = jnp.where(odd == 1, odd_place * half, even_place * half)
+        base = jnp.where(odd == n, 2 * half, half)
         lax.fori_loop(0, half // 2, functools.partial(step, base, side), 0, unroll=4)
-    if tiles_ref is not refs[-1]:
-        weights, weight_ref = refs[2 * per_side : 2 * per_side + group], refs[-1]
-        me = lax.axis_index("feat")
-        _, features = weights[0].shape
-        rows = []
-        for rank in range(group):
-            row = weights[0][...].astype(jnp.float32)
-            for m in range(1, group):
-                row = jnp.where(me ^ m == rank, weights[m][...].astype(jnp.float32), row)
-            rows.append(row)
-        weight_ref[...] = jnp.zeros_like(weight_ref)
-        weight_ref[:features, :features] = jnp.concatenate(rows, axis=0).astype(jnp.bfloat16)
-
-
-def main_kernel(group, dst, per_row, *refs):
-    rows = refs[-1].shape[0] - 1
-    batch = min(4, rows // 2)
-    sets = [[[pltpu.ACC(q)((2 * dst, 2 * LANES), jnp.float32) for _ in range(per_row // 2)] for _ in range(2)] for q in range(2)]
-    linear = [pltpu.ACC(q)((batch * LANES, 2 * LANES), jnp.float32) for q in range(2)]
-    pl.run_scoped(lambda a, b: main_body(group, dst, per_row, batch, a, b, *refs), sets, linear)
-
-
-def main_body(group, dst, per_row, batch, accs, products, neighbours_ref, *refs):
-    held, weight_ref, bias_ref, feats_ref, *ins, out_ref, sums_ref, degrees_ref = refs
-    chunk_refs = [ins[n : n + group] for n in range(0, len(ins), group)]
-    for a in [a for by_mxu in accs for by_set in by_mxu for a in by_set] + products:
+    weights = pieces[2 * per_side :]
+    me = lax.axis_index("feat")
+    features = weights[0].shape[1]
+    rows = []
+    for rank in range(group):
+        row = weights[0][...].astype(jnp.float32)
+        for m in range(1, group):
+            row = jnp.where(me ^ m == rank, weights[m][...].astype(jnp.float32), row)
+        rows.append(row)
+    weight_ref[...] = jnp.zeros_like(weight_ref)
+    weight_ref[:features, :features] = jnp.concatenate(rows, axis=0).astype(jnp.bfloat16)
+
+
+def mask_accumulators(dst, per_row):
+    shape = (2 * dst, 2 * LANES)
+    return [[[pltpu.ACC(q)(shape, jnp.float32) for _ in range(per_row // 2)] for _ in range(2)] for q in range(2)]
+
+
+def emptied(accs):
+    for a in accs:
         pltpu.matmul_pop(a)
+
+
+def sum_rows(group, dst, per_row, start, accs, neighbours_ref, held, chunk_refs, sums_ref, degrees_ref):
+    emptied([a for by_mxu in accs for by_set in by_mxu for a in by_set])
     me = lax.axis_index("feat")
-    rows = sums_ref.shape[0] - 1
-    slots, words = ins[0].shape[1:3]
+    slots, words = chunk_refs[0][0].shape[1:3]
     tiles, half = neighbours_ref.shape[1], held.shape[0] // 4
+    features = held.shape[2]
     origin = lax.axis_index("tiles") * tiles - half
-    bias = bias_ref[...]
-    features = bias.shape[1]
     pairs = per_row // 2
     one, zero = jnp.bfloat16(1), jnp.bfloat16(0)
     upper = lax.broadcasted_iota(jnp.int32, (2 * SUB, LANES), 0) >= SUB
@@ -169,7 +171,7 @@
         )
 
     def row_of(words_refs, first, row, which):
-        tile = row * per_row
+        tile = (start + row) * per_row
         count = jnp.zeros((SUB, LANES), jnp.int32)
         turn = 0
         for m in range(group):
@@ -198,31 +200,96 @@
     first = 0
     for words_refs in chunk_refs:
         size = words_refs[0].shape[0]
-
-        def step(n, carry, words_refs=words_refs, first=first):
-            for j in range(2):
-                row_of(words_refs, first, first + 2 * n + j, j)
+        count = 4 if size % 4 == 0 else 2
+
+        def step(n, carry, words_refs=words_refs, first=first, count=count):
+            for j in range(count):
+                row_of(words_refs, first, first + count * n + j, j % 2)
             return carry
 
-        lax.fori_loop(0, size // 2, step, 0)
+        lax.fori_loop(0, size // count, step, 0)
         first += size
-    sums_ref[rows] = finished(1)
-
-    for q in range(2):
-        pltpu.matmul_push_rhs(weight_ref[...], 0, q)
-    for n in range(0, rows, batch):
-        q = n // batch % 2
-        bases, wide = [], []
-        for row in range(n, n + batch):
-            scale = jnp.sqrt(degrees_ref[row] + 1.0).T[:, :1]
-            base = feats_ref[row * per_row : (row + 1) * per_row].reshape(LANES, features).astype(jnp.float32)
-            normed = ((sums_ref[row + 1] + base) / scale).astype(jnp.bfloat16)
-            bases.append(base)
-            wide.append(jnp.concatenate([normed, jnp.zeros_like(normed)], axis=1))
-        pltpu.matmul_acc_lhs(products[q], jnp.concatenate(wide, axis=0), load_staged_rhs=0 if n // batch < 2 else None)
-        linear = pltpu.matmul_pop(products[q])[:, :features] + bias
-        result = (jnp.concatenate(bases, axis=0) + jnp.maximum(linear, 0.0)).astype(jnp.bfloat16)
-        out_ref[n * per_row : (n + batch) * per_row] = result.reshape(batch * per_row, dst, features)
+    sums_ref[first] = finished(1)
+
+
+def early_kernel(group, dst, per_row, neighbours_ref, perm_ref, *refs):
+    whole = [[pltpu.ACC(q)((2 * LANES, 2 * LANES), jnp.float32) for _ in range(2)] for q in range(2)]
+
+    def body(accs, whole):
+        _, far = split(group)
+        per_side = 1 + len(far)
+        sides = [refs[n * per_side : (n + 1) * per_side] for n in range(2)]
+        held, sums_ref, degrees_ref = refs[-3:]
+        words = refs[2 * per_side : -4]
+        half = sides[0][0].shape[1]
+        odd = lax.axis_index("tiles") % 2
+        bases = [jnp.where(odd == q, 3 * half, 0) for q in range(2)]
+        emptied(whole[0] + whole[1])
+        perm = perm_ref[...]
+
+        def step(i, carry):
+            for n in range(2):
+                for q in range(2):
+                    pair = [tile_of(group, sides[q], 4 * i + 2 * n + j) for j in range(2)]
+                    pltpu.matmul_push_rhs(jnp.concatenate(pair, axis=1), n, q)
+                    pltpu.matmul_acc_lhs(whole[q][n], perm, load_staged_rhs=n)
+            for n in range(2):
+                for q in range(2):
+                    got = pltpu.matmul_pop(whole[q][n])
+                    for j in range(2):
+                        tile = got[:, j * LANES : (j + 1) * LANES]
+                        held[bases[q] + 4 * i + 2 * n + j] = tile.astype(jnp.bfloat16)
+            return carry
+
+        lax.fori_loop(0, half // 4, step, 0, unroll=2)
+        chunk_refs = [words[n : n + group] for n in range(0, len(words), group)]
+        sum_rows(group, dst, per_row, 0, accs, neighbours_ref, held, chunk_refs, sums_ref, degrees_ref)
+
+    pl.run_scoped(body, mask_accumulators(dst, per_row), whole)
+
+
+def late_kernel(group, dst, per_row, neighbours_ref, *refs):
+    def body(accs, products):
+        held, weight_ref, bias_ref, feats_ref, *words, early_sums, early_degrees = refs[:-5]
+        out_ref, sums_ref, degrees_ref, result_ref, sem = refs[-5:]
+        emptied(products)
+        features = bias_ref.shape[1]
+        bias = bias_ref[...]
+        start = early_degrees.shape[0]
+
+        def finish(start, sums_ref, degrees_ref, turn):
+            rows = degrees_ref.shape[0]
+            for n in range(0, rows, 2):
+                bases, wide = [], []
+                for row in range(n, n + 2):
+                    scale = jnp.sqrt(degrees_ref[row] + 1.0).T[:, :1]
+                    own = feats_ref[(start + row) * per_row : (start + row + 1) * per_row]
+                    base = own.reshape(LANES, features).astype(jnp.float32)
+                    normed = ((sums_ref[row + 1] + base) / scale).astype(jnp.bfloat16)
+                    bases.append(base)
+                    wide.append(jnp.concatenate([normed, jnp.zeros_like(normed)], axis=1))
+                q = n // 2 % 2
+                if n < 4:
+                    pltpu.matmul_push_rhs(weight_ref[...], 0, q)
+                lhs = jnp.concatenate(wide, axis=0)
+                pltpu.matmul_acc_lhs(products[q], lhs, load_staged_rhs=0 if n < 4 else None)
+                linear = pltpu.matmul_pop(products[q])[:, :features] + bias
+                result = (jnp.concatenate(bases, axis=0) + jnp.maximum(linear, 0.0)).astype(jnp.bfloat16)
+                at = (start + n) * per_row
+                result_ref[at : at + 2 * per_row] = result.reshape(2 * per_row, dst, features)
+            part = pl.ds(start * per_row, rows * per_row)
+            return pltpu.make_async_copy(result_ref.at[part], out_ref.at[part], sem.at[turn])
+
+        first = finish(0, early_sums, early_degrees, 0)
+        first.start()
+        sum_rows(group, dst, per_row, start, accs, neighbours_ref, held, [words], sums_ref, degrees_ref)
+        last = finish(start, sums_ref, degrees_ref, 1)
+        last.start()
+        first.wait()
+        last.wait()
+
+    products = [pltpu.ACC(q)((2 * LANES, 2 * LANES), jnp.float32) for q in range(2)]
+    pl.run_scoped(body, mask_accumulators(dst, per_row), products)
 
 
 def swap(x, group, m):
@@ -238,10 +305,10 @@
     per_row = LANES // dst
     rows = tiles // per_row
     assert half >= REACH and rows % 4 == 0 and per_row % 2 == 0 and bands % 2 == 0 and features == LANES
-    sizes = [rows // 2, rows - rows // 2]
+    sizes = [rows // 4, rows // 4, rows // 2] if rows % 8 == 0 else [rows // 2, rows // 2]
 
     shapes = [jax.ShapeDtypeStruct((n, slots, words, LANES), jnp.int16) for n in sizes for _ in range(group)]
-    block = min(sizes) * per_row
+    block = math.gcd(*sizes) * per_row
     packed = pl.pallas_call(
         lambda *refs: pack_kernel(group, dst, per_row, BITS - (words * BITS - cells), sizes, *refs),
         out_shape=shapes,
@@ -292,42 +359,52 @@
     cell = row_cells(words, cells)
     column = ((cell // dst) ^ me) * dst + cell % dst
     perm = (column[:, None] == jnp.arange(cells, dtype=jnp.int32)[None, :]).astype(jnp.bfloat16)
-    reachable_shape = jax.ShapeDtypeStruct((4 * half, cells, features), jnp.bfloat16)
-    assemble = functools.partial(
-        pl.pallas_call,
+    reachable = jax.ShapeDtypeStruct((4 * half, cells, features), jnp.bfloat16)
+    sides = inners + outers + weight_pieces
+    own_tiles, weight_wide = pl.pallas_call(
+        lambda *refs: assemble_kernel(group, *refs),
+        out_shape=[reachable, jax.ShapeDtypeStruct((2 * features, 2 * features), jnp.bfloat16)],
+        in_specs=[VMEM] * (1 + len(sides)),
+        out_specs=[VMEM] * 2,
         compiler_params=pltpu.CompilerParams(vmem_limit_bytes=4 * 2**20),
         cost_estimate=pl.CostEstimate(flops=2 * 10**9, bytes_accessed=4 * 10**6, transcendentals=0),
         name="assemble",
-    )
-    sides = inners + outers + weight_pieces
-    reachable, weight_wide = assemble(
-        lambda *refs: assemble_kernel(group, ((2, 1), (1, 2)), *refs),
-        out_shape=[reachable_shape, jax.ShapeDtypeStruct((2 * features, 2 * features), jnp.bfloat16)],
-        in_specs=[VMEM] * (1 + len(sides)),
-        out_specs=[VMEM] * 2,
     )(perm, *sides)
+
+    late = sizes[-1]
+    early = rows - late
     sides = from_inside + from_across
-    reachable = assemble(
-        lambda *refs: assemble_kernel(group, ((3, 0), (0, 3)), *refs),
-        out_shape=reachable_shape,
-        in_specs=[VMEM] * (2 + len(sides)),
-        out_specs=VMEM,
-        input_output_aliases={1 + len(sides): 0},
-    )(perm, *sides, reachable)
-
+    parts = exchanged[:-group]
+    all_tiles, early_sums, early_degrees = pl.pallas_call(
+        lambda *refs: early_kernel(group, dst, per_row, *refs),
+        out_shape=[
+            reachable,
+            jax.ShapeDtypeStruct((early + 1, LANES, features), jnp.float32),
+            jax.ShapeDtypeStruct((early, SUB, LANES), jnp.float32),
+        ],
+        in_specs=[SMEM] + [VMEM] * (2 + len(sides) + len(parts)),
+        out_specs=[VMEM] * 3,
+        input_output_aliases={2 + len(sides) + len(parts): 0},
+        compiler_params=pltpu.CompilerParams(vmem_limit_bytes=12 * 2**20),
+        cost_estimate=pl.CostEstimate(flops=10**10, bytes_accessed=10**7, transcendentals=0),
+        name="early",
+    )(neighbours.T, perm, *sides, *parts, own_tiles)
+    parts = exchanged[-group:]
     return pl.pallas_call(
-        lambda *refs: main_kernel(group, dst, per_row, *refs),
+        lambda *refs: late_kernel(group, dst, per_row, *refs),
         out_shape=jax.ShapeDtypeStruct(feats.shape, feats.dtype),
-        in_specs=[SMEM] + [VMEM] * (4 + len(exchanged)),
-        out_specs=VMEM,
+        in_specs=[SMEM] + [VMEM] * (6 + len(parts)),
+        out_specs=HBM,
         scratch_shapes=[
-            pltpu.VMEM((rows + 1, LANES, features), jnp.float32),
-            pltpu.VMEM((rows + 1, SUB, LANES), jnp.float32),
+            pltpu.VMEM((late + 1, LANES, features), jnp.float32),
+            pltpu.VMEM((late, SUB, LANES), jnp.float32),
+            pltpu.VMEM(feats.shape, jnp.bfloat16),
+            pltpu.SemaphoreType.DMA((2,)),
         ],
         compiler_params=pltpu.CompilerParams(vmem_limit_bytes=12 * 2**20),
         cost_estimate=pl.CostEstimate(flops=10**10, bytes_accessed=10**7, transcendentals=0),
-        name="main",
-    )(neighbours.T, reachable, weight_wide, bias[None, :], feats, *exchanged)
+        name="late",
+    )(neighbours.T, all_tiles, weight_wide, bias[None, :], feats, *parts, early_sums, early_degrees)
 
 
 def solution(mesh):

time: 73 us -> 81.7 us (1.12)
  the two profiles are of different devices: /device:TPU:12 before, /device:TPU:0 now
where the time goes in v2:
time: 81.7 us; the launch traced here: 81.3 us
  waiting for transfers between devices  38.8 us (47%)
  starting transfers between devices  20.4 us (25%)
  Pallas kernels  18.5 us (23%)
  local copies, waits for them, and re-layouts  3.11 us (4%)
    ppermute x16, waiting for transfers between devices, swap(): return lax.ppermute(x, 'feat', [(i, i ^ m) for i in range(group)])  38.8 us
    ppermute x16, starting transfers between devices, swap(): return lax.ppermute(x, 'feat', [(i, i ^ m) for i in range(group)])  18.7 us
    pallas_call x1, Pallas kernels, per_device(): pl.pallas_call(lambda *refs: late_kernel(group, dst, per_row, *refs), out...  5.65 us
    pallas_call x1, Pallas kernels, per_device(): pl.pallas_call(lambda *refs: early_kernel(group, dst, per_row, *refs), ou...  5.09 us
    pallas_call x1, Pallas kernels, per_device(): pl.pallas_call(lambda *refs: pack_kernel(group, dst, per_row, BITS - (wor...  4.75 us
    unnamed x34, local copies, waits for them, and re-layouts  3.11 us
    pallas_call x1, Pallas kernels, per_device(): pl.pallas_call(lambda *refs: assemble_kernel(group, *refs), out_shape=[re...  2.28 us
    ppermute x2, starting transfers between devices, per_device(): from_across.append(lax.ppermute(outers[n], 'tiles', across))  1.7 us
  transfers between devices with their start and end apart: 20, of which 10 were waited for; matrix products, arithmetic and copies ran while one was open for 0% of the time, Pallas kernels for 15%

profile of v2, /device:TPU:0, one launch (start us, length us, event | category | flops | bytes accessed | tf_op | source)
XLA Modules:
  0.0 81.3 jit_solution(3387547503950913725)
XLA Ops:
  0.0 3.0 %collective-permute-start.1 = (bf16[32,64,128]{2,1,0:T(8,128)(2,1)}, bf16[32,64,128]{2,1,0:T(8,128)(2,1)S(1)}, u32[]{:S(2)}, u32[]{:S(2)}) collective-permute-start(bf16[32,64,128]{2,1,0:T(8,128)(2,1)} %refs_4_.1), channel_id=1, source_target_pairs={{0,2},{1,3},{2,0},{3,1},{4,6},{5,7},{6,4},{7,5},{8,10},{9,11},{10,... | collective-permute-start | bytes 1572872 | tf_op jit(solution)/shard_map/ppermute | solution.py:296
  3.0 1.5 %collective-permute-start = (bf16[32,64,128]{2,1,0:T(8,128)(2,1)}, bf16[32,64,128]{2,1,0:T(8,128)(2,1)S(1)}, u32[]{:S(2)}, u32[]{:S(2)}) collective-permute-start(bf16[32,64,128]{2,1,0:T(8,128)(2,1)} %refs_4_.1), channel_id=1, source_target_pairs={{0,1},{1,0},{2,3},{3,2},{4,5},{5,4},{6,7},{7,6},{8,9},{9,8},{10,11... | collective-permute-start | bytes 1572872 | tf_op jit(solution)/shard_map/ppermute | solution.py:296
  4.5 10.6 %collective-permute-done.1.refs_3_ = bf16[32,64,128]{2,1,0:T(8,128)(2,1)S(1)} collective-permute-done((bf16[32,64,128]{2,1,0:T(8,128)(2,1)}, bf16[32,64,128]{2,1,0:T(8,128)(2,1)S(1)}, u32[]{:S(2)}, u32[]{:S(2)}) %collective-permute-start.1) | collective-permute-done | bytes 524320 | tf_op jit(solution)/shard_map/ppermute | solution.py:296
  15.1 1.5 %collective-permute-done.refs_2_ = bf16[32,64,128]{2,1,0:T(8,128)(2,1)S(1)} collective-permute-done((bf16[32,64,128]{2,1,0:T(8,128)(2,1)}, bf16[32,64,128]{2,1,0:T(8,128)(2,1)S(1)}, u32[]{:S(2)}, u32[]{:S(2)}) %collective-permute-start) | collective-permute-done | bytes 524320 | tf_op jit(solution)/shard_map/ppermute | solution.py:296
  16.6 1.0 %copy-done = bf16[32,64,128]{2,1,0:T(8,128)(2,1)S(1)} copy-done((bf16[32,64,128]{2,1,0:T(8,128)(2,1)S(1)}, bf16[32,64,128]{2,1,0:T(8,128)(2,1)}, u32[]{:S(2)}) %copy-start) | copy-done | bytes 524312
  17.6 0.7 copy-done.7
  18.3 0.8 arrange.1
  19.1 0.7 copy-done.2
  19.8 0.8 %collective-permute-start.5 = (bf16[3,16,64,128]{3,2,1,0:T(8,128)(2,1)S(1)}, bf16[3,16,64,128]{3,2,1,0:T(8,128)(2,1)S(1)}, u32[]{:S(2)}, u32[]{:S(2)}) collective-permute-start(bf16[3,16,64,128]{3,2,1,0:T(8,128)(2,1)S(1)} %get-tuple-element.28.refs_3_), channel_id=1, source_target_pairs={{4,8},{8,4},{12,16},{16,12},{20,24},{24,20},{5,9},{9,5},{13,17},{1... | collective-permute-start | bytes 2359304 | tf_op jit(solution)/shard_map/ppermute | solution.py:356
  20.7 4.7 %pack.1 = (s16[4,4,24,128]{3,2,1,0:T(8,128)(2,1)}, s16[4,4,24,128]{3,2,1,0:T(8,128)(2,1)}, s16[4,4,24,128]{3,2,1,0:T(8,128)(2,1)}, s16[4,4,24,128]{3,2,1,0:T(8,1...) custom-call(s32[32]{0:T(128)} %refs_0_.3, ...), custom_call_target="tpu_custom_call" | custom-call | flops 3000000000 | bytes 5000000 | tf_op jit(solution)/shard_map/pack/pallas_call | solution.py:312
  25.4 1.5 %collective-permute-start.8 = (s16[4,4,24,128]{3,2,1,0:T(8,128)(2,1)}, s16[4,4,24,128]{3,2,1,0:T(8,128)(2,1)S(1)}, u32[]{:S(2)}, u32[]{:S(2)}) collective-permute-start(s16[4,4,24,128]{3,2,1,0:T(8,128)(2,1)} %get-tuple-element.31), channel_id=1, source_target_pairs={{0,1},{1,0},{2,3},{3,2},{4,5},{5,4},{6,7},{7,6},{8,9},{9,8},{10,11... | collective-permute-start | bytes 294920 | tf_op jit(solution)/shard_map/ppermute | solution.py:296
  27.4 1.5 %collective-permute-start.15 = (bf16[32,128]{1,0:T(8,128)(2,1)S(1)}, bf16[32,128]{1,0:T(8,128)(2,1)S(1)}, u32[]{:S(2)}, u32[]{:S(2)}) collective-permute-start(bf16[32,128]{1,0:T(8,128)(2,1)S(1)} %copy-done.5), channel_id=1, source_target_pairs={{0,2},{1,3},{2,0},{3,1},{4,6},{5,7},{6,4},{7,5},{8,10},{9,11},{10,... | collective-permute-start | bytes 24584 | tf_op jit(solution)/shard_map/ppermute | solution.py:296
  29.0 2.9 %collective-permute-done.15.refs_7_ = bf16[32,128]{1,0:T(8,128)(2,1)S(1)} collective-permute-done((bf16[32,128]{1,0:T(8,128)(2,1)S(1)}, bf16[32,128]{1,0:T(8,128)(2,1)S(1)}, u32[]{:S(2)}, u32[]{:S(2)}) %collective-permute-start.15) | collective-permute-done | bytes 8224 | tf_op jit(solution)/shard_map/ppermute | solution.py:296
  32.4 3.1 %collective-permute-done.14.refs_6_ = bf16[32,128]{1,0:T(8,128)(2,1)S(1)} collective-permute-done((bf16[32,128]{1,0:T(8,128)(2,1)S(1)}, bf16[32,128]{1,0:T(8,128)(2,1)S(1)}, u32[]{:S(2)}, u32[]{:S(2)}) %collective-permute-start.14) | collective-permute-done | bytes 8224 | tf_op jit(solution)/shard_map/ppermute | solution.py:296
  35.5 0.7 collective-permute-start.16
  36.2 3.8 %collective-permute-done.16.refs_8_ = bf16[32,128]{1,0:T(8,128)(2,1)S(1)} collective-permute-done((bf16[32,128]{1,0:T(8,128)(2,1)S(1)}, bf16[32,128]{1,0:T(8,128)(2,1)S(1)}, u32[]{:S(2)}, u32[]{:S(2)}) %collective-permute-start.16) | collective-permute-done | bytes 8224 | tf_op jit(solution)/shard_map/ppermute | solution.py:296
  40.0 0.7 collective-permute-start.10
  40.8 1.3 %collective-permute-start.3 = (bf16[16,64,128]{2,1,0:T(8,128)(2,1)}, bf16[16,64,128]{2,1,0:T(8,128)(2,1)}, u32[]{:S(2)}, u32[]{:S(2)}) collective-permute-start(bf16[16,64,128]{2,1,0:T(8,128)(2,1)} %copy-done.2), channel_id=1, source_target_pairs={{0,2},{1,3},{2,0},{3,1},{4,6},{5,7},{6,4},{7,5},{8,10},{9,11},{10,... | collective-permute-start | bytes 786440 | tf_op jit(solution)/shard_map/ppermute | solution.py:296
  42.7 1.5 %collective-permute-start.6 = (bf16[16,64,128]{2,1,0:T(8,128)(2,1)S(1)}, bf16[16,64,128]{2,1,0:T(8,128)(2,1)}, u32[]{:S(2)}, u32[]{:S(2)}) collective-permute-start(bf16[16,64,128]{2,1,0:T(8,128)(2,1)S(1)} %get-tuple-element.29), channel_id=1, source_target_pairs={{0,1},{1,0},{2,3},{3,2},{4,5},{5,4},{6,7},{7,6},{8,9},{9,8},{10,11... | collective-permute-start | bytes 786440 | tf_op jit(solution)/shard_map/ppermute | solution.py:296
  44.2 2.7 %collective-permute-done.10.refs_9_ = s16[4,4,24,128]{3,2,1,0:T(8,128)(2,1)} collective-permute-done((s16[4,4,24,128]{3,2,1,0:T(8,128)(2,1)}, s16[4,4,24,128]{3,2,1,0:T(8,128)(2,1)}, u32[]{:S(2)}, u32[]{:S(2)}) %collective-permute-start.10) | collective-permute-done | bytes 98336 | tf_op jit(solution)/shard_map/ppermute | solution.py:296
  47.3 5.3 %collective-permute-done.11.refs_11_ = s16[4,4,24,128]{3,2,1,0:T(8,128)(2,1)S(1)} collective-permute-done((s16[4,4,24,128]{3,2,1,0:T(8,128)(2,1)}, s16[4,4,24,128]{3,2,1,0:T(8,128)(2,1)S(1)}, u32[]{:S(2)}, u32[]{:S(2)}) %collective-permute-start.11) | collective-permute-done | bytes 98336 | tf_op jit(solution)/shard_map/ppermute | solution.py:296
  52.7 0.7 collective-permute-start.12
  53.4 0.9 %collective-permute-start.7 = (bf16[16,64,128]{2,1,0:T(8,128)(2,1)}, bf16[16,64,128]{2,1,0:T(8,128)(2,1)S(1)}, u32[]{:S(2)}, u32[]{:S(2)}) collective-permute-start(bf16[16,64,128]{2,1,0:T(8,128)(2,1)} %collective-permute-done.6.refs_4_), channel_id=1, source_target_pairs={{4,8},{8,4},{12,16},{16,12},{20,24},{24,20},{5,9},{9,5},{13,17},{1... | collective-permute-start | bytes 786440 | tf_op jit(solution)/shard_map/ppermute | solution.py:356
  54.3 3.2 %collective-permute-done.12.refs_12_ = s16[4,4,24,128]{3,2,1,0:T(8,128)(2,1)S(1)} collective-permute-done((s16[4,4,24,128]{3,2,1,0:T(8,128)(2,1)}, s16[4,4,24,128]{3,2,1,0:T(8,128)(2,1)S(1)}, u32[]{:S(2)}, u32[]{:S(2)}) %collective-permute-start.12) | collective-permute-done | bytes 98336 | tf_op jit(solution)/shard_map/ppermute | solution.py:296
  57.5 1.4 %collective-permute-start.13 = (s16[4,4,24,128]{3,2,1,0:T(8,128)(2,1)}, s16[4,4,24,128]{3,2,1,0:T(8,128)(2,1)S(1)}, u32[]{:S(2)}, u32[]{:S(2)}) collective-permute-start(s16[4,4,24,128]{3,2,1,0:T(8,128)(2,1)} %get-tuple-element.37), channel_id=1, source_target_pairs={{0,3},{1,2},{2,1},{3,0},{4,7},{5,6},{6,5},{7,4},{8,11},{9,10},{10,... | collective-permute-start | bytes 294920 | tf_op jit(solution)/shard_map/ppermute | solution.py:296
  58.9 2.3 %assemble.1 = (bf16[64,256,128]{2,1,0:T(8,128)(2,1)S(1)}, bf16[256,256]{1,0:T(8,128)(2,1)S(1)}) custom-call(bf16[256,256]{1,0:T(8,128)(2,1)S(1)} %fusion.refs_0_.refs_1_, bf16[3,16,64,128]{3,2,1,0:T(8,128)(2,1)S(1)} %get-tuple-element.26.refs_1_, bf16[16,64,128]{2,1,0:T(8,128)(2,1)} %collective-permute-done.3.refs_2_, ...), custom_call_target="tpu_custom_call" | custom-call | flops 2000000000 | bytes 4000000 | tf_op jit(solution)/shard_map/assemble/pallas_call | solution.py:364
  61.1 2.5 %collective-permute-done.13.refs_13_ = s16[4,4,24,128]{3,2,1,0:T(8,128)(2,1)S(1)} collective-permute-done((s16[4,4,24,128]{3,2,1,0:T(8,128)(2,1)}, s16[4,4,24,128]{3,2,1,0:T(8,128)(2,1)S(1)}, u32[]{:S(2)}, u32[]{:S(2)}) %collective-permute-start.13) | collective-permute-done | bytes 98336 | tf_op jit(solution)/shard_map/ppermute | solution.py:296
  64.1 1.1 %collective-permute-start.18 = (s16[8,4,24,128]{3,2,1,0:T(8,128)(2,1)S(1)}, s16[8,4,24,128]{3,2,1,0:T(8,128)(2,1)S(1)}, u32[]{:S(2)}, u32[]{:S(2)}) collective-permute-start(s16[8,4,24,128]{3,2,1,0:T(8,128)(2,1)S(1)} %copy-done.15), channel_id=1, source_target_pairs={{0,2},{1,3},{2,0},{3,1},{4,6},{5,7},{6,4},{7,5},{8,10},{9,11},{10,... | collective-permute-start | bytes 589832 | tf_op jit(solution)/shard_map/ppermute | solution.py:296
  65.2 2.0 %collective-permute-start.19 = (s16[8,4,24,128]{3,2,1,0:T(8,128)(2,1)S(1)}, s16[8,4,24,128]{3,2,1,0:T(8,128)(2,1)S(1)}, u32[]{:S(2)}, u32[]{:S(2)}) collective-permute-start(s16[8,4,24,128]{3,2,1,0:T(8,128)(2,1)S(1)} %copy-done.14), channel_id=1, source_target_pairs={{0,3},{1,2},{2,1},{3,0},{4,7},{5,6},{6,5},{7,4},{8,11},{9,10},{10,... | collective-permute-start | bytes 589832 | tf_op jit(solution)/shard_map/ppermute | solution.py:296
  67.3 5.1 %early.1 = (bf16[64,256,128]{2,1,0:T(8,128)(2,1)S(1)}, f32[9,128,128]{2,1,0:T(8,128)S(1)}, f32[8,8,128]{2,1,0:T(8,128)S(1)}) custom-call(s32[16,32]{1,0:T(8,128)S(1)} %bitcast.2, bf16[256,256]{1,0:T(8,128)(2,1)S(1)} %fusion.refs_0_.refs_1_, bf16[3,16,64,128]{3,2,1,0:T(8,128)(2,1)S(1)} %collective-permute-done.2.refs_2_, ...), custom_call_target="tpu_custom_call", output_to_operand_aliasing={{0}: (14, {})} | custom-call | flops 10000000000 | bytes 10000000 | tf_op jit(solution)/shard_map/early/pallas_call | solution.py:378
  72.4 3.1 %collective-permute-done.18.refs_7_ = s16[8,4,24,128]{3,2,1,0:T(8,128)(2,1)S(1)} collective-permute-done((s16[8,4,24,128]{3,2,1,0:T(8,128)(2,1)S(1)}, s16[8,4,24,128]{3,2,1,0:T(8,128)(2,1)S(1)}, u32[]{:S(2)}, u32[]{:S(2)}) %collective-permute-start.18) | collective-permute-done | bytes 196640 | tf_op jit(solution)/shard_map/ppermute | solution.py:296
  75.5 5.7 %late.1 = bf16[32,64,128]{2,1,0:T(8,128)(2,1)} custom-call(s32[16,32]{1,0:T(8,128)S(1)} %bitcast.3, bf16[64,256,128]{2,1,0:T(8,128)(2,1)S(1)} %get-tuple-element.39.refs_1_, bf16[256,256]{1,0:T(8,128)(2,1)S(1)} %get-tuple-element.40.refs_2_, f32[1,128]{1,0:T(1,128)S(1)} %bitcast.4, bf16[32,64,128]{2,1,0:T(8,128)(2,1)S(1)} %copy-done.1, ...), custom_call_target="tpu_custom_call" | custom-call | flops 10000000000 | bytes 10000000 | tf_op jit(solution)/shard_map/late/pallas_call | solution.py:393
  (49 shorter events, 2.7 us)
Async XLA Ops:
  0.0 15.1 %collective-permute-start.1 = (bf16[32,64,128]{2,1,0:T(8,128)(2,1)}, bf16[32,64,128]{2,1,0:T(8,128)(2,1)S(1)}, u32[]{:S(2)}, u32[]{:S(2)}) collective-permute-start(bf16[32,64,128]{2,1,0:T(8,128)(2,1)} %refs_4_.1), channel_id=1, source_target_pairs={{0,2},{1,3},{2,0},{3,1},{4,6},{5,7},{6,4},{7,5},{8,10},{9,11},{10,... | collective-permute-start | bytes 1572872 | tf_op jit(solution)/shard_map/ppermute | solution.py:296
  3.0 13.6 %collective-permute-start = (bf16[32,64,128]{2,1,0:T(8,128)(2,1)}, bf16[32,64,128]{2,1,0:T(8,128)(2,1)S(1)}, u32[]{:S(2)}, u32[]{:S(2)}) collective-permute-start(bf16[32,64,128]{2,1,0:T(8,128)(2,1)} %refs_4_.1), channel_id=1, source_target_pairs={{0,1},{1,0},{2,3},{3,2},{4,5},{5,4},{6,7},{7,6},{8,9},{9,8},{10,11... | collective-permute-start | bytes 1572872 | tf_op jit(solution)/shard_map/ppermute | solution.py:296
  19.8 47.4 %collective-permute-start.2 = (bf16[3,16,64,128]{3,2,1,0:T(8,128)(2,1)S(1)}, bf16[3,16,64,128]{3,2,1,0:T(8,128)(2,1)S(1)}, u32[]{:S(2)}, u32[]{:S(2)}) collective-permute-start(bf16[3,16,64,128]{3,2,1,0:T(8,128)(2,1)S(1)} %get-tuple-element.26.refs_1_), channel_id=1, source_target_pairs={{0,4},{4,0},{8,12},{12,8},{16,20},{20,16},{24,28},{28,24},{1,5},{5... | collective-permute-start | bytes 2359304 | tf_op jit(solution)/shard_map/ppermute | solution.py:357
  19.8 27.5 %copy-start.12 = (s32[256]{0:T(256)S(1)}, s32[256]{0:T(256)}, u32[]{:S(2)}) copy-start(s32[256]{0:T(256)} %constant.11.clone) | copy-start | bytes 3076
  19.8 27.5 %copy-start.13 = (s32[256]{0:T(256)S(1)}, s32[256]{0:T(256)}, u32[]{:S(2)}) copy-start(s32[256]{0:T(256)} %constant.10.clone) | copy-start | bytes 3076
  19.8 47.4 %collective-permute-start.5 = (bf16[3,16,64,128]{3,2,1,0:T(8,128)(2,1)S(1)}, bf16[3,16,64,128]{3,2,1,0:T(8,128)(2,1)S(1)}, u32[]{:S(2)}, u32[]{:S(2)}) collective-permute-start(bf16[3,16,64,128]{3,2,1,0:T(8,128)(2,1)S(1)} %get-tuple-element.28.refs_3_), channel_id=1, source_target_pairs={{4,8},{8,4},{12,16},{16,12},{20,24},{24,20},{5,9},{9,5},{13,17},{1... | collective-permute-start | bytes 2359304 | tf_op jit(solution)/shard_map/ppermute | solution.py:356
  25.4 41.8 %copy-start.6 = (s32[32,16]{0,1:T(8,128)S(1)}, s32[32,16]{0,1:T(8,128)}, u32[]{:S(2)}) copy-start(s32[32,16]{0,1:T(8,128)} %param.12) | copy-start | bytes 6148
  25.4 15.4 %collective-permute-start.8 = (s16[4,4,24,128]{3,2,1,0:T(8,128)(2,1)}, s16[4,4,24,128]{3,2,1,0:T(8,128)(2,1)S(1)}, u32[]{:S(2)}, u32[]{:S(2)}) collective-permute-start(s16[4,4,24,128]{3,2,1,0:T(8,128)(2,1)} %get-tuple-element.31), channel_id=1, source_target_pairs={{0,1},{1,0},{2,3},{3,2},{4,5},{5,4},{6,7},{7,6},{8,9},{9,8},{10,11... | collective-permute-start | bytes 294920 | tf_op jit(solution)/shard_map/ppermute | solution.py:296
  26.9 15.1 %collective-permute-start.9 = (s16[4,4,24,128]{3,2,1,0:T(8,128)(2,1)}, s16[4,4,24,128]{3,2,1,0:T(8,128)(2,1)S(1)}, u32[]{:S(2)}, u32[]{:S(2)}) collective-permute-start(s16[4,4,24,128]{3,2,1,0:T(8,128)(2,1)} %get-tuple-element.32), channel_id=1, source_target_pairs={{0,2},{1,3},{2,0},{3,1},{4,6},{5,7},{6,4},{7,5},{8,10},{9,11},{10,... | collective-permute-start | bytes 294920 | tf_op jit(solution)/shard_map/ppermute | solution.py:296
  27.4 4.4 %collective-permute-start.15 = (bf16[32,128]{1,0:T(8,128)(2,1)S(1)}, bf16[32,128]{1,0:T(8,128)(2,1)S(1)}, u32[]{:S(2)}, u32[]{:S(2)}) collective-permute-start(bf16[32,128]{1,0:T(8,128)(2,1)S(1)} %copy-done.5), channel_id=1, source_target_pairs={{0,2},{1,3},{2,0},{3,1},{4,6},{5,7},{6,4},{7,5},{8,10},{9,11},{10,... | collective-permute-start | bytes 24584 | tf_op jit(solution)/shard_map/ppermute | solution.py:296
  31.8 3.7 %collective-permute-start.14 = (bf16[32,128]{1,0:T(8,128)(2,1)S(1)}, bf16[32,128]{1,0:T(8,128)(2,1)S(1)}, u32[]{:S(2)}, u32[]{:S(2)}) collective-permute-start(bf16[32,128]{1,0:T(8,128)(2,1)S(1)} %copy-done.5), channel_id=1, source_target_pairs={{0,1},{1,0},{2,3},{3,2},{4,5},{5,4},{6,7},{7,6},{8,9},{9,8},{10,11... | collective-permute-start | bytes 24584 | tf_op jit(solution)/shard_map/ppermute | solution.py:296
  35.5 4.5 %collective-permute-start.16 = (bf16[32,128]{1,0:T(8,128)(2,1)S(1)}, bf16[32,128]{1,0:T(8,128)(2,1)S(1)}, u32[]{:S(2)}, u32[]{:S(2)}) collective-permute-start(bf16[32,128]{1,0:T(8,128)(2,1)S(1)} %copy-done.5), channel_id=1, source_target_pairs={{0,3},{1,2},{2,1},{3,0},{4,7},{5,6},{6,5},{7,4},{8,11},{9,10},{10,... | collective-permute-start | bytes 24584 | tf_op jit(solution)/shard_map/ppermute | solution.py:296
  40.0 6.9 %collective-permute-start.10 = (s16[4,4,24,128]{3,2,1,0:T(8,128)(2,1)}, s16[4,4,24,128]{3,2,1,0:T(8,128)(2,1)}, u32[]{:S(2)}, u32[]{:S(2)}) collective-permute-start(s16[4,4,24,128]{3,2,1,0:T(8,128)(2,1)} %get-tuple-element.33), channel_id=1, source_target_pairs={{0,3},{1,2},{2,1},{3,0},{4,7},{5,6},{6,5},{7,4},{8,11},{9,10},{10,... | collective-permute-start | bytes 294920 | tf_op jit(solution)/shard_map/ppermute | solution.py:296
  40.8 12.6 %collective-permute-start.3 = (bf16[16,64,128]{2,1,0:T(8,128)(2,1)}, bf16[16,64,128]{2,1,0:T(8,128)(2,1)}, u32[]{:S(2)}, u32[]{:S(2)}) collective-permute-start(bf16[16,64,128]{2,1,0:T(8,128)(2,1)} %copy-done.2), channel_id=1, source_target_pairs={{0,2},{1,3},{2,0},{3,1},{4,6},{5,7},{6,4},{7,5},{8,10},{9,11},{10,... | collective-permute-start | bytes 786440 | tf_op jit(solution)/shard_map/ppermute | solution.py:296
  42.7 10.7 %collective-permute-start.6 = (bf16[16,64,128]{2,1,0:T(8,128)(2,1)S(1)}, bf16[16,64,128]{2,1,0:T(8,128)(2,1)}, u32[]{:S(2)}, u32[]{:S(2)}) collective-permute-start(bf16[16,64,128]{2,1,0:T(8,128)(2,1)S(1)} %get-tuple-element.29), channel_id=1, source_target_pairs={{0,1},{1,0},{2,3},{3,2},{4,5},{5,4},{6,7},{7,6},{8,9},{9,8},{10,11... | collective-permute-start | bytes 786440 | tf_op jit(solution)/shard_map/ppermute | solution.py:296
  44.2 19.5 %copy-start.16 = (s16[8,4,24,128]{3,2,1,0:T(8,128)(2,1)S(1)}, s16[8,4,24,128]{3,2,1,0:T(8,128)(2,1)}, u32[]{:S(2)}) copy-start(s16[8,4,24,128]{3,2,1,0:T(8,128)(2,1)} %get-tuple-element.42) | copy-start | bytes 589828
  44.2 19.9 %copy-start.15 = (s16[8,4,24,128]{3,2,1,0:T(8,128)(2,1)S(1)}, s16[8,4,24,128]{3,2,1,0:T(8,128)(2,1)}, u32[]{:S(2)}) copy-start(s16[8,4,24,128]{3,2,1,0:T(8,128)(2,1)} %get-tuple-element.43) | copy-start | bytes 589828
  44.2 21.0 %copy-start.14 = (s16[8,4,24,128]{3,2,1,0:T(8,128)(2,1)S(1)}, s16[8,4,24,128]{3,2,1,0:T(8,128)(2,1)}, u32[]{:S(2)}) copy-start(s16[8,4,24,128]{3,2,1,0:T(8,128)(2,1)} %get-tuple-element.44) | copy-start | bytes 589828
  44.2 23.0 %copy-start.4 = (s16[4,4,24,128]{3,2,1,0:T(8,128)(2,1)S(1)}, s16[4,4,24,128]{3,2,1,0:T(8,128)(2,1)}, u32[]{:S(2)}) copy-start(s16[4,4,24,128]{3,2,1,0:T(8,128)(2,1)} %copy-done.3) | copy-start | bytes 294916
  44.2 23.0 %copy-start.10 = (s16[4,4,24,128]{3,2,1,0:T(8,128)(2,1)S(1)}, s16[4,4,24,128]{3,2,1,0:T(8,128)(2,1)}, u32[]{:S(2)}) copy-start(s16[4,4,24,128]{3,2,1,0:T(8,128)(2,1)} %get-tuple-element.30.refs_6_) | copy-start | bytes 294916
  44.2 23.0 %copy-start.11 = (s16[4,4,24,128]{3,2,1,0:T(8,128)(2,1)S(1)}, s16[4,4,24,128]{3,2,1,0:T(8,128)(2,1)}, u32[]{:S(2)}) copy-start(s16[4,4,24,128]{3,2,1,0:T(8,128)(2,1)} %get-tuple-element.34.refs_10_) | copy-start | bytes 294916
  46.9 5.7 %collective-permute-start.11 = (s16[4,4,24,128]{3,2,1,0:T(8,128)(2,1)}, s16[4,4,24,128]{3,2,1,0:T(8,128)(2,1)S(1)}, u32[]{:S(2)}, u32[]{:S(2)}) collective-permute-start(s16[4,4,24,128]{3,2,1,0:T(8,128)(2,1)} %get-tuple-element.35), channel_id=1, source_target_pairs={{0,1},{1,0},{2,3},{3,2},{4,5},{5,4},{6,7},{7,6},{8,9},{9,8},{10,11... | collective-permute-start | bytes 294920 | tf_op jit(solution)/shard_map/ppermute | solution.py:296
  52.7 4.8 %collective-permute-start.12 = (s16[4,4,24,128]{3,2,1,0:T(8,128)(2,1)}, s16[4,4,24,128]{3,2,1,0:T(8,128)(2,1)S(1)}, u32[]{:S(2)}, u32[]{:S(2)}) collective-permute-start(s16[4,4,24,128]{3,2,1,0:T(8,128)(2,1)} %get-tuple-element.36), channel_id=1, source_target_pairs={{0,2},{1,3},{2,0},{3,1},{4,6},{5,7},{6,4},{7,5},{8,10},{9,11},{10,... | collective-permute-start | bytes 294920 | tf_op jit(solution)/shard_map/ppermute | solution.py:296
  53.3 10.7 %collective-permute-start.4 = (bf16[16,64,128]{2,1,0:T(8,128)(2,1)}, bf16[16,64,128]{2,1,0:T(8,128)(2,1)S(1)}, u32[]{:S(2)}, u32[]{:S(2)}) collective-permute-start(bf16[16,64,128]{2,1,0:T(8,128)(2,1)} %collective-permute-done.3.refs_2_), channel_id=1, source_target_pairs={{0,4},{4,0},{8,12},{12,8},{16,20},{20,16},{24,28},{28,24},{1,5},{5... | collective-permute-start | bytes 786440 | tf_op jit(solution)/shard_map/ppermute | solution.py:357
  53.4 11.8 %collective-permute-start.7 = (bf16[16,64,128]{2,1,0:T(8,128)(2,1)}, bf16[16,64,128]{2,1,0:T(8,128)(2,1)S(1)}, u32[]{:S(2)}, u32[]{:S(2)}) collective-permute-start(bf16[16,64,128]{2,1,0:T(8,128)(2,1)} %collective-permute-done.6.refs_4_), channel_id=1, source_target_pairs={{4,8},{8,4},{12,16},{16,12},{20,24},{24,20},{5,9},{9,5},{13,17},{1... | collective-permute-start | bytes 786440 | tf_op jit(solution)/shard_map/ppermute | solution.py:356
  57.5 6.2 %collective-permute-start.13 = (s16[4,4,24,128]{3,2,1,0:T(8,128)(2,1)}, s16[4,4,24,128]{3,2,1,0:T(8,128)(2,1)S(1)}, u32[]{:S(2)}, u32[]{:S(2)}) collective-permute-start(s16[4,4,24,128]{3,2,1,0:T(8,128)(2,1)} %get-tuple-element.37), channel_id=1, source_target_pairs={{0,3},{1,2},{2,1},{3,0},{4,7},{5,6},{6,5},{7,4},{8,11},{9,10},{10,... | collective-permute-start | bytes 294920 | tf_op jit(solution)/shard_map/ppermute | solution.py:296
  63.7 8.7 %collective-permute-start.17 = (s16[8,4,24,128]{3,2,1,0:T(8,128)(2,1)S(1)}, s16[8,4,24,128]{3,2,1,0:T(8,128)(2,1)S(1)}, u32[]{:S(2)}, u32[]{:S(2)}) collective-permute-start(s16[8,4,24,128]{3,2,1,0:T(8,128)(2,1)S(1)} %copy-done.16), channel_id=1, source_target_pairs={{0,1},{1,0},{2,3},{3,2},{4,5},{5,4},{6,7},{7,6},{8,9},{9,8},{10,11... | collective-permute-start | bytes 589832 | tf_op jit(solution)/shard_map/ppermute | solution.py:296
  64.1 11.4 %collective-permute-start.18 = (s16[8,4,24,128]{3,2,1,0:T(8,128)(2,1)S(1)}, s16[8,4,24,128]{3,2,1,0:T(8,128)(2,1)S(1)}, u32[]{:S(2)}, u32[]{:S(2)}) collective-permute-start(s16[8,4,24,128]{3,2,1,0:T(8,128)(2,1)S(1)} %copy-done.15), channel_id=1, source_target_pairs={{0,2},{1,3},{2,0},{3,1},{4,6},{5,7},{6,4},{7,5},{8,10},{9,11},{10,... | collective-permute-start | bytes 589832 | tf_op jit(solution)/shard_map/ppermute | solution.py:296
  65.2 10.3 %collective-permute-start.19 = (s16[8,4,24,128]{3,2,1,0:T(8,128)(2,1)S(1)}, s16[8,4,24,128]{3,2,1,0:T(8,128)(2,1)S(1)}, u32[]{:S(2)}, u32[]{:S(2)}) collective-permute-start(s16[8,4,24,128]{3,2,1,0:T(8,128)(2,1)S(1)} %copy-done.14), channel_id=1, source_target_pairs={{0,3},{1,2},{2,1},{3,0},{4,7},{5,6},{6,5},{7,4},{8,11},{9,10},{10,... | collective-permute-start | bytes 589832 | tf_op jit(solution)/shard_map/ppermute | solution.py:296
  67.2 8.3 %copy-start.1 = (bf16[32,64,128]{2,1,0:T(8,128)(2,1)S(1)}, bf16[32,64,128]{2,1,0:T(8,128)(2,1)}, u32[]{:S(2)}) copy-start(bf16[32,64,128]{2,1,0:T(8,128)(2,1)} %refs_4_.1) | copy-start | bytes 1572868
  67.2 8.3 %copy-start.8 = (f32[128]{0:T(128)S(1)}, f32[128]{0:T(128)}, u32[]{:S(2)}) copy-start(f32[128]{0:T(128)} %param.11) | copy-start | bytes 1540
  67.3 8.3 %copy-start.9 = (s16[8,4,24,128]{3,2,1,0:T(8,128)(2,1)S(1)}, s16[8,4,24,128]{3,2,1,0:T(8,128)(2,1)}, u32[]{:S(2)}) copy-start(s16[8,4,24,128]{3,2,1,0:T(8,128)(2,1)} %get-tuple-element.41.refs_5_) | copy-start | bytes 589828
  (5 other events, 10.7 us)

commit v3 on v2

--- a/solution.py
+++ b/solution.py
@@ -212,15 +212,17 @@
     sums_ref[first] = finished(1)
 
 
-def early_kernel(group, dst, per_row, neighbours_ref, perm_ref, *refs):
+def early_kernel(group, dst, per_row, table_ref, perm_ref, *refs):
     whole = [[pltpu.ACC(q)((2 * LANES, 2 * LANES), jnp.float32) for _ in range(2)] for q in range(2)]
 
     def body(accs, whole):
         _, far = split(group)
         per_side = 1 + len(far)
         sides = [refs[n * per_side : (n + 1) * per_side] for n in range(2)]
-        held, sums_ref, degrees_ref = refs[-3:]
-        words = refs[2 * per_side : -4]
+        held, sums_ref, degrees_ref, neighbours_ref, sem = refs[-5:]
+        words = refs[2 * per_side : -6]
+        table = pltpu.make_async_copy(table_ref, neighbours_ref, sem)
+        table.start()
         half = sides[0][0].shape[1]
         odd = lax.axis_index("tiles") % 2
         bases = [jnp.where(odd == q, 3 * half, 0) for q in range(2)]
@@ -242,16 +244,19 @@
             return carry
 
         lax.fori_loop(0, half // 4, step, 0, unroll=2)
+        table.wait()
         chunk_refs = [words[n : n + group] for n in range(0, len(words), group)]
         sum_rows(group, dst, per_row, 0, accs, neighbours_ref, held, chunk_refs, sums_ref, degrees_ref)
 
     pl.run_scoped(body, mask_accumulators(dst, per_row), whole)
 
 
-def late_kernel(group, dst, per_row, neighbours_ref, *refs):
+def late_kernel(group, dst, per_row, table_ref, *refs):
     def body(accs, products):
-        held, weight_ref, bias_ref, feats_ref, *words, early_sums, early_degrees = refs[:-5]
-        out_ref, sums_ref, degrees_ref, result_ref, sem = refs[-5:]
+        held, weight_ref, bias_ref, feats_ref, *words, early_sums, early_degrees = refs[:-6]
+        out_ref, sums_ref, degrees_ref, result_ref, neighbours_ref, sem = refs[-6:]
+        table = pltpu.make_async_copy(table_ref, neighbours_ref, sem.at[2])
+        table.start()
         emptied(products)
         features = bias_ref.shape[1]
         bias = bias_ref[...]
@@ -262,10 +267,10 @@
             for n in range(0, rows, 2):
                 bases, wide = [], []
                 for row in range(n, n + 2):
-                    scale = jnp.sqrt(degrees_ref[row] + 1.0).T[:, :1]
+                    scale = (1.0 / jnp.sqrt(degrees_ref[row] + 1.0)).T[:, :1]
                     own = feats_ref[(start + row) * per_row : (start + row + 1) * per_row]
                     base = own.reshape(LANES, features).astype(jnp.float32)
-                    normed = ((sums_ref[row + 1] + base) / scale).astype(jnp.bfloat16)
+                    normed = ((sums_ref[row + 1] + base) * scale).astype(jnp.bfloat16)
                     bases.append(base)
                     wide.append(jnp.concatenate([normed, jnp.zeros_like(normed)], axis=1))
                 q = n // 2 % 2
@@ -282,6 +287,7 @@
 
         first = finish(0, early_sums, early_degrees, 0)
         first.start()
+        table.wait()
         sum_rows(group, dst, per_row, start, accs, neighbours_ref, held, [words], sums_ref, degrees_ref)
         last = finish(start, sums_ref, degrees_ref, 1)
         last.start()
@@ -382,8 +388,9 @@
             jax.ShapeDtypeStruct((early + 1, LANES, features), jnp.float32),
             jax.ShapeDtypeStruct((early, SUB, LANES), jnp.float32),
         ],
-        in_specs=[SMEM] + [VMEM] * (2 + len(sides) + len(parts)),
+        in_specs=[VMEM] * (3 + len(sides) + len(parts)),
         out_specs=[VMEM] * 3,
+        scratch_shapes=[pltpu.SMEM(neighbours.shape[::-1], jnp.int32), pltpu.SemaphoreType.DMA],
         input_output_aliases={2 + len(sides) + len(parts): 0},
         compiler_params=pltpu.CompilerParams(vmem_limit_bytes=12 * 2**20),
         cost_estimate=pl.CostEstimate(flops=10**10, bytes_accessed=10**7, transcendentals=0),
@@ -393,13 +400,14 @@
     return pl.pallas_call(
         lambda *refs: late_kernel(group, dst, per_row, *refs),
         out_shape=jax.ShapeDtypeStruct(feats.shape, feats.dtype),
-        in_specs=[SMEM] + [VMEM] * (6 + len(parts)),
+        in_specs=[VMEM] * (7 + len(parts)),
         out_specs=HBM,
         scratch_shapes=[
             pltpu.VMEM((late + 1, LANES, features), jnp.float32),
             pltpu.VMEM((late, SUB, LANES), jnp.float32),
             pltpu.VMEM(feats.shape, jnp.bfloat16),
-            pltpu.SemaphoreType.DMA((2,)),
+            pltpu.SMEM(neighbours.shape[::-1], jnp.int32),
+            pltpu.SemaphoreType.DMA((3,)),
         ],
         compiler_params=pltpu.CompilerParams(vmem_limit_bytes=12 * 2**20),
         cost_estimate=pl.CostEstimate(flops=10**10, bytes_accessed=10**7, transcendentals=0),

time: 81.7 us -> 81.1 us (level)
  no operation moved by 1% of the time
where the time goes in v3:
time: 81.1 us; the launch traced here: 80.8 us
  waiting for transfers between devices  38.8 us (48%)
  starting transfers between devices  20.4 us (25%)
  Pallas kernels  18 us (22%)
  local copies, waits for them, and re-layouts  3.11 us (4%)
    ppermute x16, waiting for transfers between devices, swap(): return lax.ppermute(x, 'feat', [(i, i ^ m) for i in range(group)])  38.8 us
    ppermute x16, starting transfers between devices, swap(): return lax.ppermute(x, 'feat', [(i, i ^ m) for i in range(group)])  18.7 us
    pallas_call x1, Pallas kernels, per_device(): pl.pallas_call(lambda *refs: early_kernel(group, dst, per_row, *refs), ou...  5.1 us
    pallas_call x1, Pallas kernels, per_device(): pl.pallas_call(lambda *refs: late_kernel(group, dst, per_row, *refs), out...  5.07 us
    pallas_call x1, Pallas kernels, per_device(): pl.pallas_call(lambda *refs: pack_kernel(group, dst, per_row, BITS - (wor...  4.75 us
    unnamed x34, local copies, waits for them, and re-layouts  3.11 us
    pallas_call x1, Pallas kernels, per_device(): pl.pallas_call(lambda *refs: assemble_kernel(group, *refs), out_shape=[re...  2.28 us
    ppermute x2, starting transfers between devices, per_device(): from_across.append(lax.ppermute(outers[n], 'tiles', across))  1.7 us
  transfers between devices with their start and end apart: 20, of which 10 were waited for; matrix products, arithmetic and copies ran while one was open for 0% of the time, Pallas kernels for 15%

profile of v3, /device:TPU:0, one launch (start us, length us, event | category | flops | bytes accessed | tf_op | source)
XLA Modules:
  0.0 80.8 jit_solution(2126083171155286844)
XLA Ops:
  0.0 3.0 %collective-permute-start.1 = (bf16[32,64,128]{2,1,0:T(8,128)(2,1)}, bf16[32,64,128]{2,1,0:T(8,128)(2,1)S(1)}, u32[]{:S(2)}, u32[]{:S(2)}) collective-permute-start(bf16[32,64,128]{2,1,0:T(8,128)(2,1)} %refs_4_.1), channel_id=1, source_target_pairs={{0,2},{1,3},{2,0},{3,1},{4,6},{5,7},{6,4},{7,5},{8,10},{9,11},{10,... | collective-permute-start | bytes 1572872 | tf_op jit(solution)/shard_map/ppermute | solution.py:302
  3.0 1.5 %collective-permute-start = (bf16[32,64,128]{2,1,0:T(8,128)(2,1)}, bf16[32,64,128]{2,1,0:T(8,128)(2,1)S(1)}, u32[]{:S(2)}, u32[]{:S(2)}) collective-permute-start(bf16[32,64,128]{2,1,0:T(8,128)(2,1)} %refs_4_.1), channel_id=1, source_target_pairs={{0,1},{1,0},{2,3},{3,2},{4,5},{5,4},{6,7},{7,6},{8,9},{9,8},{10,11... | collective-permute-start | bytes 1572872 | tf_op jit(solution)/shard_map/ppermute | solution.py:302
  4.5 10.6 %collective-permute-done.1.refs_3_ = bf16[32,64,128]{2,1,0:T(8,128)(2,1)S(1)} collective-permute-done((bf16[32,64,128]{2,1,0:T(8,128)(2,1)}, bf16[32,64,128]{2,1,0:T(8,128)(2,1)S(1)}, u32[]{:S(2)}, u32[]{:S(2)}) %collective-permute-start.1) | collective-permute-done | bytes 524320 | tf_op jit(solution)/shard_map/ppermute | solution.py:302
  15.1 1.5 %collective-permute-done.refs_2_ = bf16[32,64,128]{2,1,0:T(8,128)(2,1)S(1)} collective-permute-done((bf16[32,64,128]{2,1,0:T(8,128)(2,1)}, bf16[32,64,128]{2,1,0:T(8,128)(2,1)S(1)}, u32[]{:S(2)}, u32[]{:S(2)}) %collective-permute-start) | collective-permute-done | bytes 524320 | tf_op jit(solution)/shard_map/ppermute | solution.py:302
  16.6 1.0 %copy-done = bf16[32,64,128]{2,1,0:T(8,128)(2,1)S(1)} copy-done((bf16[32,64,128]{2,1,0:T(8,128)(2,1)S(1)}, bf16[32,64,128]{2,1,0:T(8,128)(2,1)}, u32[]{:S(2)}) %copy-start) | copy-done | bytes 524312
  17.6 0.7 copy-done.7
  18.3 0.8 arrange.1
  19.1 0.7 copy-done.2
  19.8 0.8 %collective-permute-start.5 = (bf16[3,16,64,128]{3,2,1,0:T(8,128)(2,1)S(1)}, bf16[3,16,64,128]{3,2,1,0:T(8,128)(2,1)S(1)}, u32[]{:S(2)}, u32[]{:S(2)}) collective-permute-start(bf16[3,16,64,128]{3,2,1,0:T(8,128)(2,1)S(1)} %get-tuple-element.28.refs_3_), channel_id=1, source_target_pairs={{4,8},{8,4},{12,16},{16,12},{20,24},{24,20},{5,9},{9,5},{13,17},{1... | collective-permute-start | bytes 2359304 | tf_op jit(solution)/shard_map/ppermute | solution.py:362
  20.7 4.7 %pack.1 = (s16[4,4,24,128]{3,2,1,0:T(8,128)(2,1)}, s16[4,4,24,128]{3,2,1,0:T(8,128)(2,1)}, s16[4,4,24,128]{3,2,1,0:T(8,128)(2,1)}, s16[4,4,24,128]{3,2,1,0:T(8,1...) custom-call(s32[32]{0:T(128)} %refs_0_.3, ...), custom_call_target="tpu_custom_call" | custom-call | flops 3000000000 | bytes 5000000 | tf_op jit(solution)/shard_map/pack/pallas_call | solution.py:318
  25.4 1.5 %collective-permute-start.8 = (s16[4,4,24,128]{3,2,1,0:T(8,128)(2,1)}, s16[4,4,24,128]{3,2,1,0:T(8,128)(2,1)S(1)}, u32[]{:S(2)}, u32[]{:S(2)}) collective-permute-start(s16[4,4,24,128]{3,2,1,0:T(8,128)(2,1)} %get-tuple-element.31), channel_id=1, source_target_pairs={{0,1},{1,0},{2,3},{3,2},{4,5},{5,4},{6,7},{7,6},{8,9},{9,8},{10,11... | collective-permute-start | bytes 294920 | tf_op jit(solution)/shard_map/ppermute | solution.py:302
  27.4 1.5 %collective-permute-start.15 = (bf16[32,128]{1,0:T(8,128)(2,1)S(1)}, bf16[32,128]{1,0:T(8,128)(2,1)S(1)}, u32[]{:S(2)}, u32[]{:S(2)}) collective-permute-start(bf16[32,128]{1,0:T(8,128)(2,1)S(1)} %copy-done.5), channel_id=1, source_target_pairs={{0,2},{1,3},{2,0},{3,1},{4,6},{5,7},{6,4},{7,5},{8,10},{9,11},{10,... | collective-permute-start | bytes 24584 | tf_op jit(solution)/shard_map/ppermute | solution.py:302
  29.0 2.9 %collective-permute-done.15.refs_7_ = bf16[32,128]{1,0:T(8,128)(2,1)S(1)} collective-permute-done((bf16[32,128]{1,0:T(8,128)(2,1)S(1)}, bf16[32,128]{1,0:T(8,128)(2,1)S(1)}, u32[]{:S(2)}, u32[]{:S(2)}) %collective-permute-start.15) | collective-permute-done | bytes 8224 | tf_op jit(solution)/shard_map/ppermute | solution.py:302
  32.4 3.1 %collective-permute-done.14.refs_6_ = bf16[32,128]{1,0:T(8,128)(2,1)S(1)} collective-permute-done((bf16[32,128]{1,0:T(8,128)(2,1)S(1)}, bf16[32,128]{1,0:T(8,128)(2,1)S(1)}, u32[]{:S(2)}, u32[]{:S(2)}) %collective-permute-start.14) | collective-permute-done | bytes 8224 | tf_op jit(solution)/shard_map/ppermute | solution.py:302
  35.5 0.7 collective-permute-start.16
  36.2 3.8 %collective-permute-done.16.refs_8_ = bf16[32,128]{1,0:T(8,128)(2,1)S(1)} collective-permute-done((bf16[32,128]{1,0:T(8,128)(2,1)S(1)}, bf16[32,128]{1,0:T(8,128)(2,1)S(1)}, u32[]{:S(2)}, u32[]{:S(2)}) %collective-permute-start.16) | collective-permute-done | bytes 8224 | tf_op jit(solution)/shard_map/ppermute | solution.py:302
  40.0 0.7 collective-permute-start.10
  40.8 1.3 %collective-permute-start.3 = (bf16[16,64,128]{2,1,0:T(8,128)(2,1)}, bf16[16,64,128]{2,1,0:T(8,128)(2,1)}, u32[]{:S(2)}, u32[]{:S(2)}) collective-permute-start(bf16[16,64,128]{2,1,0:T(8,128)(2,1)} %copy-done.2), channel_id=1, source_target_pairs={{0,2},{1,3},{2,0},{3,1},{4,6},{5,7},{6,4},{7,5},{8,10},{9,11},{10,... | collective-permute-start | bytes 786440 | tf_op jit(solution)/shard_map/ppermute | solution.py:302
  42.7 1.5 %collective-permute-start.6 = (bf16[16,64,128]{2,1,0:T(8,128)(2,1)S(1)}, bf16[16,64,128]{2,1,0:T(8,128)(2,1)}, u32[]{:S(2)}, u32[]{:S(2)}) collective-permute-start(bf16[16,64,128]{2,1,0:T(8,128)(2,1)S(1)} %get-tuple-element.29), channel_id=1, source_target_pairs={{0,1},{1,0},{2,3},{3,2},{4,5},{5,4},{6,7},{7,6},{8,9},{9,8},{10,11... | collective-permute-start | bytes 786440 | tf_op jit(solution)/shard_map/ppermute | solution.py:302
  44.2 2.7 %collective-permute-done.10.refs_9_ = s16[4,4,24,128]{3,2,1,0:T(8,128)(2,1)} collective-permute-done((s16[4,4,24,128]{3,2,1,0:T(8,128)(2,1)}, s16[4,4,24,128]{3,2,1,0:T(8,128)(2,1)}, u32[]{:S(2)}, u32[]{:S(2)}) %collective-permute-start.10) | collective-permute-done | bytes 98336 | tf_op jit(solution)/shard_map/ppermute | solution.py:302
  47.3 5.3 %collective-permute-done.11.refs_11_ = s16[4,4,24,128]{3,2,1,0:T(8,128)(2,1)S(1)} collective-permute-done((s16[4,4,24,128]{3,2,1,0:T(8,128)(2,1)}, s16[4,4,24,128]{3,2,1,0:T(8,128)(2,1)S(1)}, u32[]{:S(2)}, u32[]{:S(2)}) %collective-permute-start.11) | collective-permute-done | bytes 98336 | tf_op jit(solution)/shard_map/ppermute | solution.py:302
  52.7 0.7 collective-permute-start.12
  53.4 0.9 %collective-permute-start.7 = (bf16[16,64,128]{2,1,0:T(8,128)(2,1)}, bf16[16,64,128]{2,1,0:T(8,128)(2,1)S(1)}, u32[]{:S(2)}, u32[]{:S(2)}) collective-permute-start(bf16[16,64,128]{2,1,0:T(8,128)(2,1)} %collective-permute-done.6.refs_4_), channel_id=1, source_target_pairs={{4,8},{8,4},{12,16},{16,12},{20,24},{24,20},{5,9},{9,5},{13,17},{1... | collective-permute-start | bytes 786440 | tf_op jit(solution)/shard_map/ppermute | solution.py:362
  54.3 3.2 %collective-permute-done.12.refs_12_ = s16[4,4,24,128]{3,2,1,0:T(8,128)(2,1)S(1)} collective-permute-done((s16[4,4,24,128]{3,2,1,0:T(8,128)(2,1)}, s16[4,4,24,128]{3,2,1,0:T(8,128)(2,1)S(1)}, u32[]{:S(2)}, u32[]{:S(2)}) %collective-permute-start.12) | collective-permute-done | bytes 98336 | tf_op jit(solution)/shard_map/ppermute | solution.py:302
  57.5 1.4 %collective-permute-start.13 = (s16[4,4,24,128]{3,2,1,0:T(8,128)(2,1)}, s16[4,4,24,128]{3,2,1,0:T(8,128)(2,1)S(1)}, u32[]{:S(2)}, u32[]{:S(2)}) collective-permute-start(s16[4,4,24,128]{3,2,1,0:T(8,128)(2,1)} %get-tuple-element.37), channel_id=1, source_target_pairs={{0,3},{1,2},{2,1},{3,0},{4,7},{5,6},{6,5},{7,4},{8,11},{9,10},{10,... | collective-permute-start | bytes 294920 | tf_op jit(solution)/shard_map/ppermute | solution.py:302
  58.9 2.3 %assemble.1 = (bf16[64,256,128]{2,1,0:T(8,128)(2,1)S(1)}, bf16[256,256]{1,0:T(8,128)(2,1)S(1)}) custom-call(bf16[256,256]{1,0:T(8,128)(2,1)S(1)} %fusion.refs_0_.refs_1_, bf16[3,16,64,128]{3,2,1,0:T(8,128)(2,1)S(1)} %get-tuple-element.26.refs_1_, bf16[16,64,128]{2,1,0:T(8,128)(2,1)} %collective-permute-done.3.refs_2_, ...), custom_call_target="tpu_custom_call" | custom-call | flops 2000000000 | bytes 4000000 | tf_op jit(solution)/shard_map/assemble/pallas_call | solution.py:370
  61.1 2.5 %collective-permute-done.13.refs_13_ = s16[4,4,24,128]{3,2,1,0:T(8,128)(2,1)S(1)} collective-permute-done((s16[4,4,24,128]{3,2,1,0:T(8,128)(2,1)}, s16[4,4,24,128]{3,2,1,0:T(8,128)(2,1)S(1)}, u32[]{:S(2)}, u32[]{:S(2)}) %collective-permute-start.13) | collective-permute-done | bytes 98336 | tf_op jit(solution)/shard_map/ppermute | solution.py:302
  64.1 1.1 %collective-permute-start.18 = (s16[8,4,24,128]{3,2,1,0:T(8,128)(2,1)S(1)}, s16[8,4,24,128]{3,2,1,0:T(8,128)(2,1)S(1)}, u32[]{:S(2)}, u32[]{:S(2)}) collective-permute-start(s16[8,4,24,128]{3,2,1,0:T(8,128)(2,1)S(1)} %copy-done.15), channel_id=1, source_target_pairs={{0,2},{1,3},{2,0},{3,1},{4,6},{5,7},{6,4},{7,5},{8,10},{9,11},{10,... | collective-permute-start | bytes 589832 | tf_op jit(solution)/shard_map/ppermute | solution.py:302
  65.2 2.0 %collective-permute-start.19 = (s16[8,4,24,128]{3,2,1,0:T(8,128)(2,1)S(1)}, s16[8,4,24,128]{3,2,1,0:T(8,128)(2,1)S(1)}, u32[]{:S(2)}, u32[]{:S(2)}) collective-permute-start(s16[8,4,24,128]{3,2,1,0:T(8,128)(2,1)S(1)} %copy-done.14), channel_id=1, source_target_pairs={{0,3},{1,2},{2,1},{3,0},{4,7},{5,6},{6,5},{7,4},{8,11},{9,10},{10,... | collective-permute-start | bytes 589832 | tf_op jit(solution)/shard_map/ppermute | solution.py:302
  67.3 5.1 %early.1 = (bf16[64,256,128]{2,1,0:T(8,128)(2,1)S(1)}, f32[9,128,128]{2,1,0:T(8,128)S(1)}, f32[8,8,128]{2,1,0:T(8,128)S(1)}) custom-call(s32[16,32]{1,0:T(8,128)S(1)} %bitcast.2, bf16[256,256]{1,0:T(8,128)(2,1)S(1)} %fusion.refs_0_.refs_1_, bf16[3,16,64,128]{3,2,1,0:T(8,128)(2,1)S(1)} %collective-permute-done.2.refs_2_, ...), custom_call_target="tpu_custom_call", output_to_operand_aliasing={{0}: (14, {})} | custom-call | flops 10000000000 | bytes 10000000 | tf_op jit(solution)/shard_map/early/pallas_call | solution.py:384
  72.4 3.1 %collective-permute-done.18.refs_7_ = s16[8,4,24,128]{3,2,1,0:T(8,128)(2,1)S(1)} collective-permute-done((s16[8,4,24,128]{3,2,1,0:T(8,128)(2,1)S(1)}, s16[8,4,24,128]{3,2,1,0:T(8,128)(2,1)S(1)}, u32[]{:S(2)}, u32[]{:S(2)}) %collective-permute-start.18) | collective-permute-done | bytes 196640 | tf_op jit(solution)/shard_map/ppermute | solution.py:302
  75.5 5.1 %late.1 = bf16[32,64,128]{2,1,0:T(8,128)(2,1)} custom-call(s32[16,32]{1,0:T(8,128)S(1)} %bitcast.3, bf16[64,256,128]{2,1,0:T(8,128)(2,1)S(1)} %get-tuple-element.39.refs_1_, bf16[256,256]{1,0:T(8,128)(2,1)S(1)} %get-tuple-element.40.refs_2_, f32[1,128]{1,0:T(1,128)S(1)} %bitcast.4, bf16[32,64,128]{2,1,0:T(8,128)(2,1)S(1)} %copy-done.1, ...), custom_call_target="tpu_custom_call" | custom-call | flops 10000000000 | bytes 10000000 | tf_op jit(solution)/shard_map/late/pallas_call | solution.py:400
  (49 shorter events, 2.7 us)
Async XLA Ops:
  0.0 15.1 %collective-permute-start.1 = (bf16[32,64,128]{2,1,0:T(8,128)(2,1)}, bf16[32,64,128]{2,1,0:T(8,128)(2,1)S(1)}, u32[]{:S(2)}, u32[]{:S(2)}) collective-permute-start(bf16[32,64,128]{2,1,0:T(8,128)(2,1)} %refs_4_.1), channel_id=1, source_target_pairs={{0,2},{1,3},{2,0},{3,1},{4,6},{5,7},{6,4},{7,5},{8,10},{9,11},{10,... | collective-permute-start | bytes 1572872 | tf_op jit(solution)/shard_map/ppermute | solution.py:302
  3.0 13.6 %collective-permute-start = (bf16[32,64,128]{2,1,0:T(8,128)(2,1)}, bf16[32,64,128]{2,1,0:T(8,128)(2,1)S(1)}, u32[]{:S(2)}, u32[]{:S(2)}) collective-permute-start(bf16[32,64,128]{2,1,0:T(8,128)(2,1)} %refs_4_.1), channel_id=1, source_target_pairs={{0,1},{1,0},{2,3},{3,2},{4,5},{5,4},{6,7},{7,6},{8,9},{9,8},{10,11... | collective-permute-start | bytes 1572872 | tf_op jit(solution)/shard_map/ppermute | solution.py:302
  19.8 47.4 %collective-permute-start.2 = (bf16[3,16,64,128]{3,2,1,0:T(8,128)(2,1)S(1)}, bf16[3,16,64,128]{3,2,1,0:T(8,128)(2,1)S(1)}, u32[]{:S(2)}, u32[]{:S(2)}) collective-permute-start(bf16[3,16,64,128]{3,2,1,0:T(8,128)(2,1)S(1)} %get-tuple-element.26.refs_1_), channel_id=1, source_target_pairs={{0,4},{4,0},{8,12},{12,8},{16,20},{20,16},{24,28},{28,24},{1,5},{5... | collective-permute-start | bytes 2359304 | tf_op jit(solution)/shard_map/ppermute | solution.py:363
  19.8 27.5 %copy-start.12 = (s32[256]{0:T(256)S(1)}, s32[256]{0:T(256)}, u32[]{:S(2)}) copy-start(s32[256]{0:T(256)} %constant.11.clone) | copy-start | bytes 3076
  19.8 27.5 %copy-start.13 = (s32[256]{0:T(256)S(1)}, s32[256]{0:T(256)}, u32[]{:S(2)}) copy-start(s32[256]{0:T(256)} %constant.10.clone) | copy-start | bytes 3076
  19.8 47.4 %collective-permute-start.5 = (bf16[3,16,64,128]{3,2,1,0:T(8,128)(2,1)S(1)}, bf16[3,16,64,128]{3,2,1,0:T(8,128)(2,1)S(1)}, u32[]{:S(2)}, u32[]{:S(2)}) collective-permute-start(bf16[3,16,64,128]{3,2,1,0:T(8,128)(2,1)S(1)} %get-tuple-element.28.refs_3_), channel_id=1, source_target_pairs={{4,8},{8,4},{12,16},{16,12},{20,24},{24,20},{5,9},{9,5},{13,17},{1... | collective-permute-start | bytes 2359304 | tf_op jit(solution)/shard_map/ppermute | solution.py:362
  25.4 41.8 %copy-start.6 = (s32[32,16]{0,1:T(8,128)S(1)}, s32[32,16]{0,1:T(8,128)}, u32[]{:S(2)}) copy-start(s32[32,16]{0,1:T(8,128)} %param.12) | copy-start | bytes 6148
  25.4 15.4 %collective-permute-start.8 = (s16[4,4,24,128]{3,2,1,0:T(8,128)(2,1)}, s16[4,4,24,128]{3,2,1,0:T(8,128)(2,1)S(1)}, u32[]{:S(2)}, u32[]{:S(2)}) collective-permute-start(s16[4,4,24,128]{3,2,1,0:T(8,128)(2,1)} %get-tuple-element.31), channel_id=1, source_target_pairs={{0,1},{1,0},{2,3},{3,2},{4,5},{5,4},{6,7},{7,6},{8,9},{9,8},{10,11... | collective-permute-start | bytes 294920 | tf_op jit(solution)/shard_map/ppermute | solution.py:302
  26.9 15.1 %collective-permute-start.9 = (s16[4,4,24,128]{3,2,1,0:T(8,128)(2,1)}, s16[4,4,24,128]{3,2,1,0:T(8,128)(2,1)S(1)}, u32[]{:S(2)}, u32[]{:S(2)}) collective-permute-start(s16[4,4,24,128]{3,2,1,0:T(8,128)(2,1)} %get-tuple-element.32), channel_id=1, source_target_pairs={{0,2},{1,3},{2,0},{3,1},{4,6},{5,7},{6,4},{7,5},{8,10},{9,11},{10,... | collective-permute-start | bytes 294920 | tf_op jit(solution)/shard_map/ppermute | solution.py:302
  27.4 4.4 %collective-permute-start.15 = (bf16[32,128]{1,0:T(8,128)(2,1)S(1)}, bf16[32,128]{1,0:T(8,128)(2,1)S(1)}, u32[]{:S(2)}, u32[]{:S(2)}) collective-permute-start(bf16[32,128]{1,0:T(8,128)(2,1)S(1)} %copy-done.5), channel_id=1, source_target_pairs={{0,2},{1,3},{2,0},{3,1},{4,6},{5,7},{6,4},{7,5},{8,10},{9,11},{10,... | collective-permute-start | bytes 24584 | tf_op jit(solution)/shard_map/ppermute | solution.py:302
  31.8 3.7 %collective-permute-start.14 = (bf16[32,128]{1,0:T(8,128)(2,1)S(1)}, bf16[32,128]{1,0:T(8,128)(2,1)S(1)}, u32[]{:S(2)}, u32[]{:S(2)}) collective-permute-start(bf16[32,128]{1,0:T(8,128)(2,1)S(1)} %copy-done.5), channel_id=1, source_target_pairs={{0,1},{1,0},{2,3},{3,2},{4,5},{5,4},{6,7},{7,6},{8,9},{9,8},{10,11... | collective-permute-start | bytes 24584 | tf_op jit(solution)/shard_map/ppermute | solution.py:302
  35.5 4.5 %collective-permute-start.16 = (bf16[32,128]{1,0:T(8,128)(2,1)S(1)}, bf16[32,128]{1,0:T(8,128)(2,1)S(1)}, u32[]{:S(2)}, u32[]{:S(2)}) collective-permute-start(bf16[32,128]{1,0:T(8,128)(2,1)S(1)} %copy-done.5), channel_id=1, source_target_pairs={{0,3},{1,2},{2,1},{3,0},{4,7},{5,6},{6,5},{7,4},{8,11},{9,10},{10,... | collective-permute-start | bytes 24584 | tf_op jit(solution)/shard_map/ppermute | solution.py:302
  40.0 6.9 %collective-permute-start.10 = (s16[4,4,24,128]{3,2,1,0:T(8,128)(2,1)}, s16[4,4,24,128]{3,2,1,0:T(8,128)(2,1)}, u32[]{:S(2)}, u32[]{:S(2)}) collective-permute-start(s16[4,4,24,128]{3,2,1,0:T(8,128)(2,1)} %get-tuple-element.33), channel_id=1, source_target_pairs={{0,3},{1,2},{2,1},{3,0},{4,7},{5,6},{6,5},{7,4},{8,11},{9,10},{10,... | collective-permute-start | bytes 294920 | tf_op jit(solution)/shard_map/ppermute | solution.py:302
  40.8 12.6 %collective-permute-start.3 = (bf16[16,64,128]{2,1,0:T(8,128)(2,1)}, bf16[16,64,128]{2,1,0:T(8,128)(2,1)}, u32[]{:S(2)}, u32[]{:S(2)}) collective-permute-start(bf16[16,64,128]{2,1,0:T(8,128)(2,1)} %copy-done.2), channel_id=1, source_target_pairs={{0,2},{1,3},{2,0},{3,1},{4,6},{5,7},{6,4},{7,5},{8,10},{9,11},{10,... | collective-permute-start | bytes 786440 | tf_op jit(solution)/shard_map/ppermute | solution.py:302
  42.7 10.7 %collective-permute-start.6 = (bf16[16,64,128]{2,1,0:T(8,128)(2,1)S(1)}, bf16[16,64,128]{2,1,0:T(8,128)(2,1)}, u32[]{:S(2)}, u32[]{:S(2)}) collective-permute-start(bf16[16,64,128]{2,1,0:T(8,128)(2,1)S(1)} %get-tuple-element.29), channel_id=1, source_target_pairs={{0,1},{1,0},{2,3},{3,2},{4,5},{5,4},{6,7},{7,6},{8,9},{9,8},{10,11... | collective-permute-start | bytes 786440 | tf_op jit(solution)/shard_map/ppermute | solution.py:302
  44.2 19.5 %copy-start.16 = (s16[8,4,24,128]{3,2,1,0:T(8,128)(2,1)S(1)}, s16[8,4,24,128]{3,2,1,0:T(8,128)(2,1)}, u32[]{:S(2)}) copy-start(s16[8,4,24,128]{3,2,1,0:T(8,128)(2,1)} %get-tuple-element.42) | copy-start | bytes 589828
  44.2 19.9 %copy-start.15 = (s16[8,4,24,128]{3,2,1,0:T(8,128)(2,1)S(1)}, s16[8,4,24,128]{3,2,1,0:T(8,128)(2,1)}, u32[]{:S(2)}) copy-start(s16[8,4,24,128]{3,2,1,0:T(8,128)(2,1)} %get-tuple-element.43) | copy-start | bytes 589828
  44.2 21.0 %copy-start.14 = (s16[8,4,24,128]{3,2,1,0:T(8,128)(2,1)S(1)}, s16[8,4,24,128]{3,2,1,0:T(8,128)(2,1)}, u32[]{:S(2)}) copy-start(s16[8,4,24,128]{3,2,1,0:T(8,128)(2,1)} %get-tuple-element.44) | copy-start | bytes 589828
  44.2 23.0 %copy-start.4 = (s16[4,4,24,128]{3,2,1,0:T(8,128)(2,1)S(1)}, s16[4,4,24,128]{3,2,1,0:T(8,128)(2,1)}, u32[]{:S(2)}) copy-start(s16[4,4,24,128]{3,2,1,0:T(8,128)(2,1)} %copy-done.3) | copy-start | bytes 294916
  44.2 23.0 %copy-start.10 = (s16[4,4,24,128]{3,2,1,0:T(8,128)(2,1)S(1)}, s16[4,4,24,128]{3,2,1,0:T(8,128)(2,1)}, u32[]{:S(2)}) copy-start(s16[4,4,24,128]{3,2,1,0:T(8,128)(2,1)} %get-tuple-element.30.refs_6_) | copy-start | bytes 294916
  44.2 23.0 %copy-start.11 = (s16[4,4,24,128]{3,2,1,0:T(8,128)(2,1)S(1)}, s16[4,4,24,128]{3,2,1,0:T(8,128)(2,1)}, u32[]{:S(2)}) copy-start(s16[4,4,24,128]{3,2,1,0:T(8,128)(2,1)} %get-tuple-element.34.refs_10_) | copy-start | bytes 294916
  46.9 5.7 %collective-permute-start.11 = (s16[4,4,24,128]{3,2,1,0:T(8,128)(2,1)}, s16[4,4,24,128]{3,2,1,0:T(8,128)(2,1)S(1)}, u32[]{:S(2)}, u32[]{:S(2)}) collective-permute-start(s16[4,4,24,128]{3,2,1,0:T(8,128)(2,1)} %get-tuple-element.35), channel_id=1, source_target_pairs={{0,1},{1,0},{2,3},{3,2},{4,5},{5,4},{6,7},{7,6},{8,9},{9,8},{10,11... | collective-permute-start | bytes 294920 | tf_op jit(solution)/shard_map/ppermute | solution.py:302
  52.7 4.8 %collective-permute-start.12 = (s16[4,4,24,128]{3,2,1,0:T(8,128)(2,1)}, s16[4,4,24,128]{3,2,1,0:T(8,128)(2,1)S(1)}, u32[]{:S(2)}, u32[]{:S(2)}) collective-permute-start(s16[4,4,24,128]{3,2,1,0:T(8,128)(2,1)} %get-tuple-element.36), channel_id=1, source_target_pairs={{0,2},{1,3},{2,0},{3,1},{4,6},{5,7},{6,4},{7,5},{8,10},{9,11},{10,... | collective-permute-start | bytes 294920 | tf_op jit(solution)/shard_map/ppermute | solution.py:302
  53.3 10.7 %collective-permute-start.4 = (bf16[16,64,128]{2,1,0:T(8,128)(2,1)}, bf16[16,64,128]{2,1,0:T(8,128)(2,1)S(1)}, u32[]{:S(2)}, u32[]{:S(2)}) collective-permute-start(bf16[16,64,128]{2,1,0:T(8,128)(2,1)} %collective-permute-done.3.refs_2_), channel_id=1, source_target_pairs={{0,4},{4,0},{8,12},{12,8},{16,20},{20,16},{24,28},{28,24},{1,5},{5... | collective-permute-start | bytes 786440 | tf_op jit(solution)/shard_map/ppermute | solution.py:363
  53.4 11.8 %collective-permute-start.7 = (bf16[16,64,128]{2,1,0:T(8,128)(2,1)}, bf16[16,64,128]{2,1,0:T(8,128)(2,1)S(1)}, u32[]{:S(2)}, u32[]{:S(2)}) collective-permute-start(bf16[16,64,128]{2,1,0:T(8,128)(2,1)} %collective-permute-done.6.refs_4_), channel_id=1, source_target_pairs={{4,8},{8,4},{12,16},{16,12},{20,24},{24,20},{5,9},{9,5},{13,17},{1... | collective-permute-start | bytes 786440 | tf_op jit(solution)/shard_map/ppermute | solution.py:362
  57.5 6.2 %collective-permute-start.13 = (s16[4,4,24,128]{3,2,1,0:T(8,128)(2,1)}, s16[4,4,24,128]{3,2,1,0:T(8,128)(2,1)S(1)}, u32[]{:S(2)}, u32[]{:S(2)}) collective-permute-start(s16[4,4,24,128]{3,2,1,0:T(8,128)(2,1)} %get-tuple-element.37), channel_id=1, source_target_pairs={{0,3},{1,2},{2,1},{3,0},{4,7},{5,6},{6,5},{7,4},{8,11},{9,10},{10,... | collective-permute-start | bytes 294920 | tf_op jit(solution)/shard_map/ppermute | solution.py:302
  63.7 8.7 %collective-permute-start.17 = (s16[8,4,24,128]{3,2,1,0:T(8,128)(2,1)S(1)}, s16[8,4,24,128]{3,2,1,0:T(8,128)(2,1)S(1)}, u32[]{:S(2)}, u32[]{:S(2)}) collective-permute-start(s16[8,4,24,128]{3,2,1,0:T(8,128)(2,1)S(1)} %copy-done.16), channel_id=1, source_target_pairs={{0,1},{1,0},{2,3},{3,2},{4,5},{5,4},{6,7},{7,6},{8,9},{9,8},{10,11... | collective-permute-start | bytes 589832 | tf_op jit(solution)/shard_map/ppermute | solution.py:302
  64.1 11.4 %collective-permute-start.18 = (s16[8,4,24,128]{3,2,1,0:T(8,128)(2,1)S(1)}, s16[8,4,24,128]{3,2,1,0:T(8,128)(2,1)S(1)}, u32[]{:S(2)}, u32[]{:S(2)}) collective-permute-start(s16[8,4,24,128]{3,2,1,0:T(8,128)(2,1)S(1)} %copy-done.15), channel_id=1, source_target_pairs={{0,2},{1,3},{2,0},{3,1},{4,6},{5,7},{6,4},{7,5},{8,10},{9,11},{10,... | collective-permute-start | bytes 589832 | tf_op jit(solution)/shard_map/ppermute | solution.py:302
  65.2 10.3 %collective-permute-start.19 = (s16[8,4,24,128]{3,2,1,0:T(8,128)(2,1)S(1)}, s16[8,4,24,128]{3,2,1,0:T(8,128)(2,1)S(1)}, u32[]{:S(2)}, u32[]{:S(2)}) collective-permute-start(s16[8,4,24,128]{3,2,1,0:T(8,128)(2,1)S(1)} %copy-done.14), channel_id=1, source_target_pairs={{0,3},{1,2},{2,1},{3,0},{4,7},{5,6},{6,5},{7,4},{8,11},{9,10},{10,... | collective-permute-start | bytes 589832 | tf_op jit(solution)/shard_map/ppermute | solution.py:302
  67.2 8.3 %copy-start.1 = (bf16[32,64,128]{2,1,0:T(8,128)(2,1)S(1)}, bf16[32,64,128]{2,1,0:T(8,128)(2,1)}, u32[]{:S(2)}) copy-start(bf16[32,64,128]{2,1,0:T(8,128)(2,1)} %refs_4_.1) | copy-start | bytes 1572868
  67.2 8.3 %copy-start.8 = (f32[128]{0:T(128)S(1)}, f32[128]{0:T(128)}, u32[]{:S(2)}) copy-start(f32[128]{0:T(128)} %param.11) | copy-start | bytes 1540
  67.3 8.3 %copy-start.9 = (s16[8,4,24,128]{3,2,1,0:T(8,128)(2,1)S(1)}, s16[8,4,24,128]{3,2,1,0:T(8,128)(2,1)}, u32[]{:S(2)}) copy-start(s16[8,4,24,128]{3,2,1,0:T(8,128)(2,1)} %get-tuple-element.41.refs_5_) | copy-start | bytes 589828
  (5 other events, 10.7 us)
